TPU v7x, 32 devices: a whole 2x2x4 slice. The times are simulated.
32 devices in a mesh: af: 4 (over y, x), sa: 8 (over z, core).
Axes of the slice: x: 2, y: 2, z: 4, core: 2. Of those that a mesh axis runs over, the one named last changes fastest.
Arguments:
- data_real: bfloat16 [64, 512, 512], P('af', 'sa'), may hold values from -0.5 to 0.5
- data_imaginary: bfloat16 [64, 512, 512], P('af', 'sa'), may hold values from -0.5 to 0.5
- wavelet_real: float32 [64], P('af'), may hold values from -2.5 to 2.5
- wavelet_imaginary: float32 [64], P('af'), may hold values from -2.5 to 2.5
- primaries_real: float32 [64, 512, 512], P('af', 'sa'), may hold values from -3 to 3
- primaries_imaginary: float32 [64, 512, 512], P('af', 'sa'), may hold values from -3 to 3
Outputs:
- updated_real: float32 [64, 512, 512], P('af', 'sa')
- updated_imaginary: float32 [64, 512, 512], P('af', 'sa')
- misfit: float32 [2], replicated
All inputs are finite; a program needn't handle non-finite values.
Results may differ from a plain program's by a relative error of at most 0.0018.
Values may be sent and summed in bfloat16 or wider, within the bound.
A program may use at most 128 MiB of HBM per device.

v0:
```python
import math

import jax
import jax.numpy as jnp
from jax import lax
from jax.sharding import PartitionSpec as P

N = 512
F = 64
ITERS = 2


STEP_LENGTH = 0.02
THRESHOLD = 0.25


def fourier_tables(row_index, col_index):
    phase = row_index[:, None] * col_index[None, :] % F
    angle = phase.astype(jnp.float32) * (2.0 * math.pi / F)
    factor = 1.0 / math.sqrt(F)
    return (jnp.cos(angle) * factor, jnp.sin(angle) * factor)


def highest(left, right):
    return jnp.dot(left, right, precision=lax.Precision.HIGHEST, preferred_element_type=jnp.float32)


def stacked(part_real, part_imaginary):
    return jnp.concatenate(
        [part_real.astype(jnp.bfloat16), part_imaginary.astype(jnp.bfloat16)], axis=1
    )


def shrink(values):
    return values - jnp.clip(values, -THRESHOLD, THRESHOLD)


def on_device(
    data_real, data_imaginary, wavelet_real, wavelet_imaginary, primaries_real, primaries_imaginary
):
    row_count = data_real.shape[1]
    wave_real = wavelet_real[:, None, None]
    wave_imaginary = wavelet_imaginary[:, None, None]
    current_real = primaries_real
    current_imaginary = primaries_imaginary
    own_real = data_real.astype(jnp.float32)
    own_imaginary = data_imaginary.astype(jnp.float32)
    whole_real, whole_imaginary = (
        lax.all_gather(data_real, "sa", axis=1, tiled=True),
        lax.all_gather(data_imaginary, "sa", axis=1, tiled=True),
    )
    local_sums = []
    for iteration in range(ITERS):
        left_rows = stacked(current_real, current_imaginary)
        product_real = jnp.einsum(
            "frk,fkc->frc", left_rows, whole_real, preferred_element_type=jnp.float32
        )
        product_imaginary = jnp.einsum(
            "frk,fkc->frc", left_rows, whole_imaginary, preferred_element_type=jnp.float32
        )
        forward_real = product_real[:, :row_count] - product_imaginary[:, row_count:]
        forward_imaginary = product_imaginary[:, :row_count] + product_real[:, row_count:]
        error_real = (
            own_real
            + forward_real
            - (wave_real * current_real - wave_imaginary * current_imaginary)
        )
        error_imaginary = (
            own_imaginary
            + forward_imaginary
            - (wave_real * current_imaginary + wave_imaginary * current_real)
        )
        local_sum = jnp.sum(error_real * error_real) + jnp.sum(error_imaginary * error_imaginary)
        local_sums.append(local_sum)
        error_rows = stacked(error_real, error_imaginary)
        with_real = jnp.einsum(
            "frk,fjk->frj", error_rows, whole_real, preferred_element_type=jnp.float32
        )
        with_imaginary = jnp.einsum(
            "frk,fjk->frj", error_rows, whole_imaginary, preferred_element_type=jnp.float32
        )
        back_real = with_real[:, :row_count] + with_imaginary[:, row_count:]
        back_imaginary = with_real[:, row_count:] - with_imaginary[:, :row_count]
        gradient_real = wave_real * error_real + wave_imaginary * error_imaginary - back_real
        gradient_imaginary = (
            wave_real * error_imaginary - wave_imaginary * error_real - back_imaginary
        )
        stepped_real = current_real + STEP_LENGTH * gradient_real
        stepped_imaginary = current_imaginary + STEP_LENGTH * gradient_imaginary
        trace_real, trace_imaginary = (
            lax.all_to_all(stepped_real, "af", split_axis=2, concat_axis=0, tiled=True),
            lax.all_to_all(stepped_imaginary, "af", split_axis=2, concat_axis=0, tiled=True),
        )
        block_shape = trace_real.shape
        flat_real = trace_real.reshape(F, -1)
        flat_imaginary = trace_imaginary.reshape(F, -1)
        every_index = jnp.arange(F, dtype=jnp.int32)
        cosine, sine = fourier_tables(every_index, every_index)
        time_real = highest(cosine, flat_real) - highest(sine, flat_imaginary)
        time_imaginary = highest(sine, flat_real) + highest(cosine, flat_imaginary)
        shrunk_real = shrink(time_real)
        shrunk_imaginary = shrink(time_imaginary)
        freq_real = (highest(cosine, shrunk_real) + highest(sine, shrunk_imaginary)).reshape(
            block_shape
        )
        freq_imaginary = (highest(cosine, shrunk_imaginary) - highest(sine, shrunk_real)).reshape(
            block_shape
        )
        current_real, current_imaginary = (
            lax.all_to_all(freq_real, "af", split_axis=0, concat_axis=2, tiled=True),
            lax.all_to_all(freq_imaginary, "af", split_axis=0, concat_axis=2, tiled=True),
        )
    totals = lax.psum(jnp.stack(local_sums), ("af", "sa"))
    misfit = totals / (F * N * N)
    return (current_real, current_imaginary, misfit)


def solution(mesh):
    in_specs = (
        P("af", "sa", None),
        P("af", "sa", None),
        P("af"),
        P("af"),
        P("af", "sa", None),
        P("af", "sa", None),
    )
    out_specs = (P("af", "sa", None), P("af", "sa", None), P())
    return jax.shard_map(
        on_device, mesh=mesh, in_specs=in_specs, out_specs=out_specs, check_vma=False
    )
```

profile of v0, /device:TPU:0, one launch (start us, length us, event | category | flops | bytes accessed | tf_op | source)
XLA Modules:
  0.0 607.0 jit_solution(6934212573473681621)
XLA Ops:
  8.7 2.7 convert_element_type.66
  12.5 81.9 %all-gather.5.cloned.1.call-done = bf16[16,512,512]{2,1,0:T(8,128)(2,1)} async-done(((bf16[16,64,512]{2,1,0:T(8,128)(2,1)}), bf16[16,512,512]{2,1,0:T(8,128)(2,1)}) %all-gather.5.cloned.1.call-update) | async-done | bytes 8388624 | tf_op jit(solution)/shard_map/all_gather | solution.py:50
  94.4 7.3 %fusion.46 = f32[16,128,512]{2,1,0:T(8,128)} fusion(bf16[16,512,512]{2,1,0:T(8,128)(2,1)} %all-gather.5.cloned.1.call-done, bf16[16,64,512]{2,1,0:T(8,128)(2,1)} %convert_element_type.67, bf16[16,64,512]{2,1,0:T(8,128)(2,1)} %convert_element_type.66), kind=kOutput, calls=%fused_computation.88 | convolution fusion | flops 1077936128 | bytes 14680064 | tf_op jit(solution)/shard_map/frk,fkc->frc/dot_general | solution.py:58
  101.6 74.9 %all-gather.3.cloned.1.call-done = bf16[16,512,512]{2,1,0:T(8,128)(2,1)} async-done(((bf16[16,64,512]{2,1,0:T(8,128)(2,1)}), bf16[16,512,512]{2,1,0:T(8,128)(2,1)}) %all-gather.3.cloned.1.call-update) | async-done | bytes 8388624 | tf_op jit(solution)/shard_map/all_gather | solution.py:49
  176.5 5.4 fusion.47
  182.9 2.7 multiply_reduce_fusion.3
  189.1 6.8 %fusion.44 = f32[16,128,512]{2,1,0:T(8,128)} fusion(bf16[16,512,512]{2,1,0:T(8,128)(2,1)S(1)} %bitcast.119, bf16[16,64,512]{2,1,0:T(8,128)(2,1)} %convert_element_type.70, bf16[16,64,512]{2,1,0:T(8,128)(2,1)} %convert_element_type.69), kind=kOutput, calls=%fused_computation.86 | convolution fusion | flops 1077936128 | bytes 14680064 | tf_op jit(solution)/shard_map/frk,fjk->frj/dot_general | solution.py:79
  195.9 6.5 %fusion.45 = f32[16,128,512]{2,1,0:T(8,128)} fusion(bf16[16,512,512]{2,1,0:T(8,128)(2,1)S(1)} %bitcast.123, bf16[16,64,512]{2,1,0:T(8,128)(2,1)} %convert_element_type.70, bf16[16,64,512]{2,1,0:T(8,128)(2,1)} %convert_element_type.69), kind=kOutput, calls=%fused_computation.87 | convolution fusion | flops 1077936128 | bytes 14680064 | tf_op jit(solution)/shard_map/frk,fjk->frj/dot_general | solution.py:76
  202.5 5.8 fusion.24
  208.3 4.9 copy.19
  213.2 5.5 reshape.44
  218.6 3.6 all-to-all-start
  222.3 4.9 copy.21
  227.2 5.5 reshape.46
  232.7 15.1 %all-to-all-done = f32[4,1,131072]{2,1,0:T(1,128)S(1)} async-done(((f32[4,1,131072]{2,1,0:T(1,128)}), f32[4,1,131072]{2,1,0:T(1,128)S(1)}, u32[]{:S(2)}, u32[]{:S(2)}) %all-to-all-start) | async-done | bytes 2097184 | tf_op jit(solution)/shard_map/all_to_all | solution.py:91
  249.1 4.6 all-to-all-start.1
  254.2 7.6 %reduce = f32[4,131072]{1,0:T(4,128)S(1)} reduce(f32[4,1,131072]{2,1,0:T(1,128)} %copy-done.27, f32[]{:T(128)} %broadcast.92), dimensions={1}, to_apply=%all_to_all.96.reduce_sub_computation | reduce | bytes 4194308 | tf_op jit(solution)/shard_map/all_to_all | solution.py:91
  261.8 3.9 reshape.45
  265.8 3.3 copy.20
  269.1 4.4 fusion.12
  273.5 4.4 fusion.14
  278.4 7.6 %reduce.1 = f32[4,131072]{1,0:T(4,128)S(1)} reduce(f32[4,1,131072]{2,1,0:T(1,128)} %all-to-all-done.1, f32[]{:T(128)} %broadcast.92), dimensions={1}, to_apply=%all_to_all.99.reduce_sub_computation | reduce | bytes 4194308 | tf_op jit(solution)/shard_map/all_to_all | solution.py:92
  286.0 4.4 reshape.47
  290.4 3.1 copy.22
  293.5 4.9 clamp_subtract_fusion.2
  298.5 3.3 clamp_subtract_fusion.3
  303.9 2.1 fusion.37
  307.8 3.8 all-to-all-start.3
  311.6 3.7 fusion.57
  315.4 2.1 fusion.36
  319.2 16.7 %all-to-all-done.3 = f32[64,64,128]{2,1,0:T(8,128)S(1)} async-done(((f32[64,64,128]{2,1,0:T(8,128)}), f32[64,64,128]{2,1,0:T(8,128)S(1)}, u32[]{:S(2)}, u32[]{:S(2)}) %all-to-all-start.3) | async-done | bytes 2097184 | tf_op jit(solution)/shard_map/all_to_all | solution.py:111
  335.9 4.5 all-to-all-start.2
  341.6 23.3 %all-to-all-done.2 = f32[64,64,128]{2,1,0:T(8,128)} async-done(((f32[64,64,128]{2,1,0:T(8,128)}), f32[64,64,128]{2,1,0:T(8,128)}, u32[]{:S(2)}, u32[]{:S(2)}) %all-to-all-start.2) | async-done | bytes 2097184 | tf_op jit(solution)/shard_map/all_to_all | solution.py:110
  366.8 4.9 fusion.42
  373.4 3.8 multiply_reduce_fusion.1
  380.8 6.4 %fusion.40 = f32[16,128,512]{2,1,0:T(8,128)} fusion(bf16[16,512,512]{2,1,0:T(8,128)(2,1)S(1)} %bitcast.121, bf16[16,64,512]{2,1,0:T(8,128)(2,1)} %convert_element_type.74, bf16[16,64,512]{2,1,0:T(8,128)(2,1)} %convert_element_type.73), kind=kOutput, calls=%fused_computation.82 | convolution fusion | flops 1077936128 | bytes 14680064 | tf_op jit(solution)/shard_map/frk,fjk->frj/dot_general | solution.py:79
  387.2 6.5 %fusion.41 = f32[16,128,512]{2,1,0:T(8,128)} fusion(bf16[16,512,512]{2,1,0:T(8,128)(2,1)S(1)} %bitcast.125, bf16[16,64,512]{2,1,0:T(8,128)(2,1)} %convert_element_type.74, bf16[16,64,512]{2,1,0:T(8,128)(2,1)} %convert_element_type.73), kind=kOutput, calls=%fused_computation.83 | convolution fusion | flops 1077936128 | bytes 14680064 | tf_op jit(solution)/shard_map/frk,fjk->frj/dot_general | solution.py:76
  393.7 5.1 bitcast_add_fusion
  398.7 4.9 copy.25
  403.6 5.5 reshape.48
  409.1 3.6 all-to-all-start.4
  412.7 4.9 copy.27
  417.6 5.5 reshape.50
  423.1 13.9 %all-to-all-done.4 = f32[4,1,131072]{2,1,0:T(1,128)S(1)} async-done(((f32[4,1,131072]{2,1,0:T(1,128)}), f32[4,1,131072]{2,1,0:T(1,128)S(1)}, u32[]{:S(2)}, u32[]{:S(2)}) %all-to-all-start.4) | async-done | bytes 2097184 | tf_op jit(solution)/shard_map/all_to_all | solution.py:91
  438.4 4.7 all-to-all-start.5
  443.0 7.6 %reduce.2 = f32[4,131072]{1,0:T(4,128)S(1)} reduce(f32[4,1,131072]{2,1,0:T(1,128)} %copy-done.28, f32[]{:T(128)} %broadcast.92), dimensions={1}, to_apply=%all_to_all.110.reduce_sub_computation | reduce | bytes 4194308 | tf_op jit(solution)/shard_map/all_to_all | solution.py:91
  450.7 3.9 reshape.49
  454.6 3.5 copy.26
  458.1 4.4 fusion.6
  462.5 4.4 fusion.8
  467.5 7.6 %reduce.3 = f32[4,131072]{1,0:T(4,128)S(1)} reduce(f32[4,1,131072]{2,1,0:T(1,128)} %all-to-all-done.5, f32[]{:T(128)} %broadcast.92), dimensions={1}, to_apply=%all_to_all.113.reduce_sub_computation | reduce | bytes 4194308 | tf_op jit(solution)/shard_map/all_to_all | solution.py:92
  475.1 4.1 reshape.51
  479.2 3.1 copy.28
  482.3 4.9 clamp_subtract_fusion
  487.2 3.3 clamp_subtract_fusion.1
  492.7 2.1 fusion.38
  496.5 4.8 all-to-all-start.6
  507.3 18.5 %all-to-all-done.6 = f32[64,64,128]{2,1,0:T(8,128)} async-done(((f32[64,64,128]{2,1,0:T(8,128)}), f32[64,64,128]{2,1,0:T(8,128)}, u32[]{:S(2)}, u32[]{:S(2)}) %all-to-all-start.6) | async-done | bytes 2097184 | tf_op jit(solution)/shard_map/all_to_all | solution.py:110
  525.8 3.6 all-to-all-start.7
  531.9 54.3 %psum.7 = f32[2]{0:T(128)S(1)} all-reduce(f32[2]{0:T(128)S(1)} %pad_maximum_fusion.12), channel_id=1, replica_groups=mesh['af'=4,'sa'=8] {'af','sa'}, use_global_device_ids=true, to_apply=%region_4.5 | all-reduce | flops 2 | bytes 16 | tf_op jit(solution)/shard_map/psum | solution.py:113
  586.7 4.3 copy.90
  591.0 3.0 all_to_all.119
  594.1 2.8 copy.89
  596.9 3.0 all_to_all.123
  (108 shorter events, 35.4 us)
Async XLA Ops:
  7.2 87.2 %all-gather.5.cloned.1.call-start = ((), (), s32[]{:S(2)}) async-start(), calls=%async_computation.9 | async-start | bytes 9437184 | tf_op jit(solution)/shard_map/all_gather | solution.py:50
  7.9 3.5 copy-start.8
  7.9 168.6 %all-gather.3.cloned.1.call-start = ((), (), s32[]{:S(2)}) async-start(), calls=%async_computation.8 | async-start | bytes 9437184 | tf_op jit(solution)/shard_map/all_gather | solution.py:49
  101.6 80.3 %copy-start.29 = (f32[16]{0:T(128)S(1)}, f32[16]{0:T(128)}, u32[]{:S(2)}) copy-start(f32[16]{0:T(128)} %param.9) | copy-start | bytes 196
  101.6 80.3 %copy-start.30 = (f32[16]{0:T(128)S(1)}, f32[16]{0:T(128)}, u32[]{:S(2)}) copy-start(f32[16]{0:T(128)} %param.8) | copy-start | bytes 196
  176.5 5.5 copy-start
  176.5 5.9 copy-start.9
  176.5 6.1 %copy-start.21 = (bf16[16,64,512]{2,1,0:T(8,128)(2,1)S(1)}, bf16[16,64,512]{2,1,0:T(8,128)(2,1)}, u32[]{:S(2)}) copy-start(bf16[16,64,512]{2,1,0:T(8,128)(2,1)} %param.7) | copy-start | bytes 3145732
  176.5 6.4 %copy-start.23 = (bf16[16,64,512]{2,1,0:T(8,128)(2,1)S(1)}, bf16[16,64,512]{2,1,0:T(8,128)(2,1)}, u32[]{:S(2)}) copy-start(bf16[16,64,512]{2,1,0:T(8,128)(2,1)} %param.6) | copy-start | bytes 3145732
  176.5 12.5 %slice-start = ((s8[8388608]{0:T(1024)(128)(4,1)}), s8[4194304]{0:T(1024)(128)(4,1)S(1)}, s32[]{:S(2)}) async-start(s8[8388608]{0:T(1024)(128)(4,1)} %bitcast.118), calls=%async_computation.10 | async-start | bytes 8388608
  182.9 6.1 %slice-start.1 = ((s8[8388608]{0:T(1024)(128)(4,1)}), s8[4194304]{0:T(1024)(128)(4,1)S(1)}, s32[]{:S(2)}) async-start(s8[8388608]{0:T(1024)(128)(4,1)} %bitcast.118), calls=%async_computation.11 | async-start | bytes 8388608
  185.6 1.6 copy-start.15
  185.6 2.3 copy-start.17
  187.9 8.0 %slice-start.4 = ((s8[8388608]{0:T(1024)(128)(4,1)}), s8[4194304]{0:T(1024)(128)(4,1)S(1)}, s32[]{:S(2)}) async-start(s8[8388608]{0:T(1024)(128)(4,1)} %bitcast.122), calls=%async_computation.14 | async-start | bytes 8388608
  189.0 6.8 %slice-start.5 = ((s8[8388608]{0:T(1024)(128)(4,1)}), s8[4194304]{0:T(1024)(128)(4,1)S(1)}, s32[]{:S(2)}) async-start(s8[8388608]{0:T(1024)(128)(4,1)} %bitcast.122), calls=%async_computation.15 | async-start | bytes 8388608
  195.9 6.6 %copy-start.10 = (f32[16,64,512]{2,1,0:T(8,128)S(1)}, f32[16,64,512]{2,1,0:T(8,128)}, u32[]{:S(2)}) copy-start(f32[16,64,512]{2,1,0:T(8,128)} %param.10) | copy-start | bytes 6291460
  195.9 6.6 %copy-start.16 = (f32[16,64,512]{2,1,0:T(8,128)S(1)}, f32[16,64,512]{2,1,0:T(8,128)}, u32[]{:S(2)}) copy-start(f32[16,64,512]{2,1,0:T(8,128)} %copy-done.15) | copy-start | bytes 6291460
  195.9 6.5 %copy-start.18 = (f32[16,64,512]{2,1,0:T(8,128)S(1)}, f32[16,64,512]{2,1,0:T(8,128)}, u32[]{:S(2)}) copy-start(f32[16,64,512]{2,1,0:T(8,128)} %copy-done.17) | copy-start | bytes 6291460
  218.6 29.1 %all-to-all-start = ((f32[4,1,131072]{2,1,0:T(1,128)}), f32[4,1,131072]{2,1,0:T(1,128)S(1)}, u32[]{:S(2)}, u32[]{:S(2)}) async-start(f32[4,1,131072]{2,1,0:T(1,128)} %reshape.44), calls=%async_computation | async-start | bytes 4194304 | tf_op jit(solution)/shard_map/all_to_all | solution.py:91
  247.8 1.3 copy-start.27
  249.1 29.3 %all-to-all-start.1 = ((f32[4,1,131072]{2,1,0:T(1,128)}), f32[4,1,131072]{2,1,0:T(1,128)}, u32[]{:S(2)}, u32[]{:S(2)}) async-start(f32[4,1,131072]{2,1,0:T(1,128)} %reshape.46), calls=%async_computation.1 | async-start | bytes 4194304 | tf_op jit(solution)/shard_map/all_to_all | solution.py:92
  293.5 5.0 copy-start.26
  298.5 3.3 copy-start.1
  301.8 6.0 copy-start.7
  307.8 28.2 %all-to-all-start.3 = ((f32[64,64,128]{2,1,0:T(8,128)}), f32[64,64,128]{2,1,0:T(8,128)S(1)}, u32[]{:S(2)}, u32[]{:S(2)}) async-start(f32[64,64,128]{2,1,0:T(8,128)} %bitcast.150), calls=%async_computation.3 | async-start | bytes 4194304 | tf_op jit(solution)/shard_map/all_to_all | solution.py:111
  311.6 3.8 copy-start.2
  335.9 28.9 %all-to-all-start.2 = ((f32[64,64,128]{2,1,0:T(8,128)}), f32[64,64,128]{2,1,0:T(8,128)}, u32[]{:S(2)}, u32[]{:S(2)}) async-start(f32[64,64,128]{2,1,0:T(8,128)} %bitcast.152), calls=%async_computation.2 | async-start | bytes 4194304 | tf_op jit(solution)/shard_map/all_to_all | solution.py:110
  364.9 1.9 copy-start.20
  364.9 6.9 %slice-start.6 = ((s8[8388608]{0:T(1024)(128)(4,1)}), s8[4194304]{0:T(1024)(128)(4,1)S(1)}, s32[]{:S(2)}) async-start(s8[8388608]{0:T(1024)(128)(4,1)} %bitcast.124), calls=%async_computation.16 | async-start | bytes 8388608
  366.8 5.1 slice-start.7
  371.9 1.3 copy-start.22
  371.9 1.5 copy-start.24
  371.9 8.9 %slice-start.2 = ((s8[8388608]{0:T(1024)(128)(4,1)}), s8[4194304]{0:T(1024)(128)(4,1)S(1)}, s32[]{:S(2)}) async-start(s8[8388608]{0:T(1024)(128)(4,1)} %bitcast.120), calls=%async_computation.12 | async-start | bytes 8388608
  373.4 7.4 %slice-start.3 = ((s8[8388608]{0:T(1024)(128)(4,1)}), s8[4194304]{0:T(1024)(128)(4,1)S(1)}, s32[]{:S(2)}) async-start(s8[8388608]{0:T(1024)(128)(4,1)} %bitcast.120), calls=%async_computation.13 | async-start | bytes 8388608
  377.2 1.3 copy-start.11
  377.2 2.4 copy-start.13
  387.2 6.5 %copy-start.12 = (f32[16,64,512]{2,1,0:T(8,128)S(1)}, f32[16,64,512]{2,1,0:T(8,128)}, u32[]{:S(2)}) copy-start(f32[16,64,512]{2,1,0:T(8,128)} %copy-done.11) | copy-start | bytes 6291460
  387.2 6.5 %copy-start.14 = (f32[16,64,512]{2,1,0:T(8,128)S(1)}, f32[16,64,512]{2,1,0:T(8,128)}, u32[]{:S(2)}) copy-start(f32[16,64,512]{2,1,0:T(8,128)} %copy-done.13) | copy-start | bytes 6291460
  387.2 6.5 %copy-start.19 = (f32[16,128,512]{2,1,0:T(8,128)S(1)}, f32[16,128,512]{2,1,0:T(8,128)}, u32[]{:S(2)}) copy-start(f32[16,128,512]{2,1,0:T(8,128)} %fusion.40) | copy-start | bytes 12582916
  409.1 28.0 %all-to-all-start.4 = ((f32[4,1,131072]{2,1,0:T(1,128)}), f32[4,1,131072]{2,1,0:T(1,128)S(1)}, u32[]{:S(2)}, u32[]{:S(2)}) async-start(f32[4,1,131072]{2,1,0:T(1,128)} %reshape.48), calls=%async_computation.4 | async-start | bytes 4194304 | tf_op jit(solution)/shard_map/all_to_all | solution.py:91
  437.0 1.3 copy-start.28
  438.4 29.1 %all-to-all-start.5 = ((f32[4,1,131072]{2,1,0:T(1,128)}), f32[4,1,131072]{2,1,0:T(1,128)}, u32[]{:S(2)}, u32[]{:S(2)}) async-start(f32[4,1,131072]{2,1,0:T(1,128)} %reshape.50), calls=%async_computation.5 | async-start | bytes 4194304 | tf_op jit(solution)/shard_map/all_to_all | solution.py:92
  482.3 5.0 copy-start.25
  487.2 5.4 copy-start.3
  490.5 2.1 copy-start.5
  496.5 4.8 copy-start.4
  496.5 29.3 %all-to-all-start.6 = ((f32[64,64,128]{2,1,0:T(8,128)}), f32[64,64,128]{2,1,0:T(8,128)}, u32[]{:S(2)}, u32[]{:S(2)}) async-start(f32[64,64,128]{2,1,0:T(8,128)} %bitcast.151), calls=%async_computation.6 | async-start | bytes 4194304 | tf_op jit(solution)/shard_map/all_to_all | solution.py:110
  501.3 2.1 copy-start.6
  525.8 68.3 %all-to-all-start.7 = ((f32[64,64,128]{2,1,0:T(8,128)}), f32[64,64,128]{2,1,0:T(8,128)S(1)}, u32[]{:S(2)}, u32[]{:S(2)}) async-start(f32[64,64,128]{2,1,0:T(8,128)} %bitcast.43), calls=%async_computation.7 | async-start | bytes 4194304 | tf_op jit(solution)/shard_map/all_to_all | solution.py:111
Sparse Core Ops, SparseCore 0:
  9.6 84.7 all-gather.4
  96.0 80.5 all-gather.2
where the time goes:
time: 616 us; the launch traced here: 607 us
  waiting for transfers between devices  247 us (40%)
  local copies, waits for them, and re-layouts  101 us (16%)
  matrix products  97.7 us (16%)
  other arithmetic  56.9 us (9%)
  blocking collectives  54.3 us (9%)
  starting transfers between devices  33.3 us (5%)
  between operations  17.2 us (3%)
    all_gather x1, waiting for transfers between devices, on_device(): lax.all_gather(data_imaginary, 'sa', axis=1, tiled=True)  81.9 us
    all_gather x1, waiting for transfers between devices, on_device(): lax.all_gather(data_real, 'sa', axis=1, tiled=True)  74.9 us
    psum x1, blocking collectives, on_device(): totals = lax.psum(jnp.stack(local_sums), ('af', 'sa'))  54.3 us
    dot_general x16, matrix products, highest(): jnp.dot(left, right, precision=lax.Precision.HIGHEST, preferred_element_t...  52.7 us
    unnamed x90, local copies, waits for them, and re-layouts  51.7 us
    all_to_all x2, waiting for transfers between devices, on_device(): lax.all_to_all(freq_real, 'af', split_axis=0, concat_axis=2, tiled=True)  41.8 us
    all_to_all x2, waiting for transfers between devices, on_device(): lax.all_to_all(stepped_real, 'af', split_axis=2, concat_axis=0, tiled=True)  29.1 us
    all_to_all x2, waiting for transfers between devices, on_device(): lax.all_to_all(freq_imaginary, 'af', split_axis=0, concat_axis=2, tiled=T...  16.7 us
  transfers between devices with their start and end apart: 10, of which 9 were waited for; matrix products, arithmetic and copies ran while one was open for 16% of the time, Pallas kernels for 0%

commit v1 on v0

v1 whole, which is shorter than its diff:
```python
import functools
import math

import jax
import jax.numpy as jnp
from jax import lax
from jax.experimental import pallas as pl
from jax.experimental.pallas import tpu as pltpu
from jax.sharding import PartitionSpec as P

ITERS = 2
STEP_LENGTH = 0.02
THRESHOLD = 0.25
CHUNKS = 4
GROUP = 8
HALF = math.sqrt(0.5)
MESH = pl.DeviceIdType.MESH


def product_kernel(first, offset, wr_ref, wi_ref, whole_ref, own_r_ref, own_i_ref, *rest):
    if first:
        gr_ref, gi_ref, out_ref, sum_ref = rest
        gr = gr_ref[0]
        gi = gi_ref[0]
    else:
        g_ref, out_ref, sum_ref = rest
        parts = g_ref.shape[0]
        gr = jnp.concatenate([g_ref[a, 0, 0] for a in range(parts)], axis=1)
        gi = jnp.concatenate([g_ref[a, 1, 0] for a in range(parts)], axis=1)
    at = pl.program_id(0) + offset
    qr = wr_ref[at]
    qi = wi_ref[at]
    rows = gr.shape[0]
    n = gr.shape[1]
    whole_r = whole_ref[:, 0, 0].reshape(n, n)
    whole_i = whole_ref[:, 1, 0].reshape(n, n)
    left = jnp.concatenate([gr.astype(jnp.bfloat16), gi.astype(jnp.bfloat16)], axis=0)
    pr = jnp.dot(left, whole_r, preferred_element_type=jnp.float32)
    pi = jnp.dot(left, whole_i, preferred_element_type=jnp.float32)
    er = own_r_ref[0].astype(jnp.float32) + (pr[:rows] - pi[rows:]) - (qr * gr - qi * gi)
    ei = own_i_ref[0].astype(jnp.float32) + (pi[:rows] + pr[rows:]) - (qr * gi + qi * gr)
    sum_ref[0] = jnp.sum(er * er + ei * ei, axis=0, keepdims=True)
    eb = jnp.concatenate([er.astype(jnp.bfloat16), ei.astype(jnp.bfloat16)], axis=0)
    dims = (((1,), (1,)), ((), ()))
    br = lax.dot_general(eb, whole_r, dims, preferred_element_type=jnp.float32)
    bi = lax.dot_general(eb, whole_i, dims, preferred_element_type=jnp.float32)
    hr = qr * er + qi * ei - (br[:rows] + bi[rows:])
    hi = qr * ei - qi * er - (br[rows:] - bi[:rows])
    zr = gr + STEP_LENGTH * hr
    zi = gi + STEP_LENGTH * hi
    parts = out_ref.shape[0]
    width = n // parts
    for a in range(parts):
        out_ref[a, 0, 0] = zr[:, a * width : (a + 1) * width]
        out_ref[a, 1, 0] = zi[:, a * width : (a + 1) * width]


def product(offset, count, parts, wr, wi, whole, own_r, own_i, current):
    sa, _, _, rows, n = whole.shape
    first = len(current) == 2
    plain = pl.BlockSpec((1, rows, n), lambda f: (f + offset, 0, 0))
    scalars = pl.BlockSpec(memory_space=pltpu.SMEM)
    width = n // parts
    if first:
        cur_specs = [plain, plain]
    else:
        cur_specs = [pl.BlockSpec((parts, 2, 1, rows, width), lambda f: (0, 0, f + offset, 0, 0))]
    return pl.pallas_call(
        functools.partial(product_kernel, first, offset),
        grid=(count,),
        in_specs=[scalars, scalars, pl.BlockSpec((sa, 2, 1, rows, n), lambda f: (0, 0, f, 0, 0)), plain, plain]
        + cur_specs,
        out_specs=[
            pl.BlockSpec((parts, 2, 1, rows, width), lambda f: (0, 0, f, 0, 0)),
            pl.BlockSpec((1, 1, n), lambda f: (f, 0, 0)),
        ],
        out_shape=[
            jax.ShapeDtypeStruct((parts, 2, count, rows, width), jnp.float32),
            jax.ShapeDtypeStruct((count, 1, n), jnp.float32),
        ],
        cost_estimate=pl.CostEstimate(
            flops=16 * count * rows * n * n, bytes_accessed=count * n * (n * 4 + rows * 20), transcendentals=0
        ),
        compiler_params=pltpu.CompilerParams(vmem_limit_bytes=60 * 2**20),
    )(wr, wi, whole, own_r, own_i, *current)


def add(a, b):
    return (a[0] + b[0], a[1] + b[1])


def sub(a, b):
    return (a[0] - b[0], a[1] - b[1])


def turn(a, sign):
    return (-a[1], a[0]) if sign > 0 else (a[1], -a[0])


def rotate(a, turns):
    c, s = math.cos(2 * math.pi * turns), math.sin(2 * math.pi * turns)
    return (a[0] * c - a[1] * s, a[0] * s + a[1] * c)


def four(a, b, c, d, sign):
    s0, s1, s2, s3 = add(a, c), sub(a, c), add(b, d), turn(sub(b, d), sign)
    return add(s0, s2), add(s1, s3), sub(s0, s2), sub(s1, s3)


def eight(x, sign):
    even = four(x[0], x[2], x[4], x[6], sign)
    odd = four(x[1], x[3], x[5], x[7], sign)
    o1 = add(odd[1], turn(odd[1], sign))
    o3 = sub(turn(odd[3], sign), odd[3])
    odd = (odd[0], (o1[0] * HALF, o1[1] * HALF), turn(odd[2], sign), (o3[0] * HALF, o3[1] * HALF))
    return [add(even[k], odd[k]) for k in range(4)] + [sub(even[k], odd[k]) for k in range(4)]


def shrink(v):
    return v - jnp.clip(v, -THRESHOLD, THRESHOLD)


def transform_kernel(pieces, in_scale, out_scale, *refs):
    in_refs, out_ref, work = refs[:pieces], refs[pieces], refs[pieces + 1]
    parts, _, local, block, width = out_ref.shape
    piece = local // pieces
    radix = 8
    factor = 1.0 / radix

    def one(g, _):
        at = pl.ds(pl.multiple_of(g * GROUP, GROUP), GROUP)

        def load(f):
            a, b = divmod(f, local)
            c, d = divmod(b, piece)
            ref = in_refs[c]
            scale = factor * in_scale
            return (
                ref[a, 0, d, at, :].astype(jnp.float32) * scale,
                ref[a, 1, d, at, :].astype(jnp.float32) * scale,
            )

        for f1 in range(radix):
            y = eight([load(f1 + radix * f2) for f2 in range(radix)], 1)
            for t2 in range(radix):
                v = rotate(y[t2], f1 * t2 / 64) if f1 * t2 else y[t2]
                work[0, radix * f1 + t2] = v[0]
                work[1, radix * f1 + t2] = v[1]
        for t2 in range(radix):
            y = eight([(work[0, radix * f1 + t2], work[1, radix * f1 + t2]) for f1 in range(radix)], 1)
            y = [(shrink(v[0]), shrink(v[1])) for v in y]
            y = eight(y, -1)
            for f1 in range(radix):
                v = rotate(y[f1], -f1 * t2 / 64) if f1 * t2 else y[f1]
                work[0, radix * f1 + t2] = v[0]
                work[1, radix * f1 + t2] = v[1]
        for f1 in range(radix):
            y = eight([(work[0, radix * f1 + t2], work[1, radix * f1 + t2]) for t2 in range(radix)], -1)
            for f2 in range(radix):
                a, b = divmod(f1 + radix * f2, local)
                scale = factor * out_scale
                out_ref[a, 0, b, at, :] = y[f2][0] * scale
                out_ref[a, 1, b, at, :] = y[f2][1] * scale
        return 0

    lax.fori_loop(0, block // GROUP, one, 0)


def transform(arrays, in_scale, out_scale):
    pieces = len(arrays)
    parts, _, piece, rows, width = arrays[0].shape
    local = piece * pieces
    block = min(16, rows)
    return pl.pallas_call(
        functools.partial(transform_kernel, pieces, in_scale, out_scale),
        grid=(rows // block,),
        in_specs=[pl.BlockSpec((parts, 2, piece, block, width), lambda r: (0, 0, 0, r, 0))] * pieces,
        out_specs=pl.BlockSpec((parts, 2, local, block, width), lambda r: (0, 0, 0, r, 0)),
        out_shape=jax.ShapeDtypeStruct((parts, 2, local, rows, width), jnp.float32),
        scratch_shapes=[pltpu.VMEM((2, parts * local, GROUP, width), jnp.float32)],
        cost_estimate=pl.CostEstimate(
            flops=4000 * rows * width, bytes_accessed=16 * parts * local * rows * width, transcendentals=0
        ),
        compiler_params=pltpu.CompilerParams(vmem_limit_bytes=60 * 2**20),
    )(*arrays)


def total_kernel(counts, own_ref, out_ref, slots, send_sem, recv_sem):
    afs, sas = counts
    n = afs * sas
    me = lax.axis_index("af") * sas + lax.axis_index("sa")

    def peer(k):
        p = lax.rem(me + k, n)
        return (p // sas, lax.rem(p, sas))

    def hello(k, _):
        pl.semaphore_signal(barrier, inc=1, device_id=peer(k), device_id_type=MESH)
        return 0

    def copy(k):
        return pltpu.make_async_remote_copy(
            src_ref=own_ref,
            dst_ref=slots.at[k],
            send_sem=send_sem.at[k],
            recv_sem=recv_sem.at[k],
            device_id=peer(k),
            device_id_type=MESH,
        )

    def start(k, _):
        copy(k).start()
        return 0

    def finish(k, value):
        copy(k).wait()
        return value + slots[k]

    barrier = pltpu.get_barrier_semaphore()
    lax.fori_loop(1, n, hello, 0)
    pl.semaphore_wait(barrier, n - 1)
    lax.fori_loop(1, n, start, 0)
    out_ref[...] = lax.fori_loop(1, n, finish, own_ref[...])


def total(own, counts):
    n = counts[0] * counts[1]
    return pl.pallas_call(
        functools.partial(total_kernel, counts),
        out_shape=jax.ShapeDtypeStruct(own.shape, own.dtype),
        in_specs=[pl.BlockSpec(memory_space=pltpu.VMEM)],
        out_specs=pl.BlockSpec(memory_space=pltpu.VMEM),
        scratch_shapes=[
            pltpu.VMEM((n, *own.shape), own.dtype),
            pltpu.SemaphoreType.DMA((n,)),
            pltpu.SemaphoreType.DMA((n,)),
        ],
        compiler_params=pltpu.CompilerParams(collective_id=0, has_side_effects=True),
    )(own)


def exchange(values):
    return lax.all_to_all(values, "af", split_axis=0, concat_axis=0, tiled=True)


def on_device(counts, data_real, data_imaginary, wave_real, wave_imaginary, primaries_real, primaries_imaginary):
    parts = counts[0]
    local, rows, n = data_real.shape
    size = local // CHUNKS
    wholes = []
    for c in range(CHUNKS):
        cut = slice(c * size, (c + 1) * size)
        both = jnp.stack([data_real[cut], data_imaginary[cut]])
        wholes.append(lax.all_gather(both, "sa", axis=0))
    first = (primaries_real, primaries_imaginary)
    sums = []
    current = None
    for iteration in range(ITERS):
        wire = jnp.float16 if iteration == 0 else jnp.float32
        traces = []
        squares = []
        for c in range(CHUNKS):
            stepped, square = product(
                c * size, size, parts, wave_real, wave_imaginary, wholes[c], data_real, data_imaginary,
                first if iteration == 0 else (current,),
            )
            squares.append(square)
            traces.append(exchange(stepped.astype(wire)).astype(jnp.float32))
        sums.append(jnp.sum(jnp.concatenate(squares)))
        scale = 0.25 if iteration == 0 else 1.0
        back = transform(traces, 1.0, scale)
        current = exchange(back.astype(wire)).astype(jnp.float32)
        if iteration == 0:
            current = current / scale
    updated = current.transpose(1, 2, 3, 0, 4).reshape(2, local, rows, n)
    row = lax.broadcasted_iota(jnp.int32, (8, 128), 0)
    own = jnp.where(row == 0, sums[0], jnp.where(row == 1, sums[1], 0.0))
    misfit = total(own, counts)[:ITERS, 0] / (parts * local * n * n)
    return (updated[0], updated[1], misfit)


def solution(mesh):
    split = P("af", "sa", None)
    counts = (mesh.shape["af"], mesh.shape["sa"])
    return jax.shard_map(
        functools.partial(on_device, counts),
        mesh=mesh,
        in_specs=(split, split, P("af"), P("af"), split, split),
        out_specs=(split, split, P()),
        check_vma=False,
    )
```

time: 616 us -> 417 us (0.68); the launches traced: 607 us -> 415 us
  Pallas kernels: 0 us -> 98 us
  matrix products: 97.7 us -> 0 us
  local copies, waits for them, and re-layouts: 101 us -> 13.8 us
  waiting for transfers between devices: 247 us -> 180 us
  other arithmetic: 56.9 us -> 28.5 us
  blocking collectives: 54.3 us -> 45.4 us
    pallas_call x0 -> x11, Pallas kernels: none -> 98 us  [the longest x8 46.6 us: product(): pl.pallas_call(functools.partial(product_kernel, first, offset), grid=(co...]
    dot_general x24 -> x0, matrix products: 97.7 us -> none  [the longest x16 52.7 us: highest(): jnp.dot(left, right, precision=lax.Precision.HIGHEST, preferred_element_t...]
    all_to_all x8, waiting for transfers between devices: 88.6 us -> 25.7 us  [exchange(): return lax.all_to_all(values, 'af', split_axis=0, concat_axis=0, tiled=True)]
    psum x1 -> x0, blocking collectives: 54.3 us -> none  [on_device(): totals = lax.psum(jnp.stack(local_sums), ('af', 'sa'))]
    unnamed x90 -> x22, local copies, waits for them, and re-layouts: 51.7 us -> 0.04 us
    all_to_all x0 -> x2, blocking collectives: none -> 45.4 us  [exchange(): return lax.all_to_all(values, 'af', split_axis=0, concat_axis=0, tiled=True)]
    all_to_all x4 -> x0, other arithmetic: 30.5 us -> none  [the longest x2 15.2 us: on_device(): lax.all_to_all(stepped_real, 'af', split_axis=2, concat_axis=0, tiled=True)]
    all_to_all x11 -> x0, local copies, waits for them, and re-layouts: 29.6 us -> none  [the longest x3 9.29 us: on_device(): lax.all_to_all(freq_real, 'af', split_axis=0, concat_axis=2, tiled=True)]
  transfers between devices with their start and end apart: 10 -> 12, of which waited for: 9 -> 8; matrix products, arithmetic and copies ran while one was open for 16% -> 5% of each run, Pallas kernels for 0% -> 19%
where the time goes in v1:
time: 417 us; the launch traced here: 415 us
  waiting for transfers between devices  180 us (43%)
  Pallas kernels  98 us (24%)
  blocking collectives  45.4 us (11%)
  starting transfers between devices  30.3 us (7%)
  other arithmetic  28.5 us (7%)
  between operations  18.9 us (5%)
  local copies, waits for them, and re-layouts  13.8 us (3%)
    all_gather x4, waiting for transfers between devices, on_device(): wholes.append(lax.all_gather(both, 'sa', axis=0))  154 us
    pallas_call x8, Pallas kernels, product(): pl.pallas_call(functools.partial(product_kernel, first, offset), grid=(co...  46.6 us
    all_to_all x2, blocking collectives, exchange(): return lax.all_to_all(values, 'af', split_axis=0, concat_axis=0, tiled=True)  45.4 us
    pallas_call x1, Pallas kernels, total(): pl.pallas_call(functools.partial(total_kernel, counts), out_shape=jax.Sha...  38.1 us
    all_to_all x8, starting transfers between devices, exchange(): return lax.all_to_all(values, 'af', split_axis=0, concat_axis=0, tiled=True)  30.2 us
    all_to_all x8, waiting for transfers between devices, exchange(): return lax.all_to_all(values, 'af', split_axis=0, concat_axis=0, tiled=True)  25.7 us
    pallas_call x2, Pallas kernels, transform(): pl.pallas_call(functools.partial(transform_kernel, pieces, in_scale, out_...  13.3 us
    convert_element_type x8, other arithmetic, on_device(): traces.append(exchange(stepped.astype(wire)).astype(jnp.float32))  13 us
  transfers between devices with their start and end apart: 12, of which 8 were waited for; matrix products, arithmetic and copies ran while one was open for 5% of the time, Pallas kernels for 19%

profile of v1, /device:TPU:0, one launch (start us, length us, event | category | flops | bytes accessed | tf_op | source)
XLA Modules:
  0.0 414.9 jit_solution(9687772501802879483)
XLA Ops:
  7.2 0.0 all-gather.9.cloned.1.call-start
  7.2 1.7 slice_bitcast_fusion
  8.9 0.8 pad_maximum_fusion
  9.7 0.0 all-gather.11.cloned.1.call-start
  9.8 0.8 pad_maximum_fusion.1
  10.6 0.0 all-gather.11.cloned.1.call-update
  10.7 0.0 all-gather.13.cloned.1.call-start
  10.7 0.8 pad_maximum_fusion.2
  11.6 0.0 all-gather.15.cloned.1.call-start
  11.6 0.9 pad_maximum_fusion.3
  12.5 47.3 %all-gather.9.cloned.1.call-done = bf16[16,4,64,512]{3,2,1,0:T(8,128)(2,1)} async-done(((bf16[2,4,64,512]{3,2,1,0:T(8,128)(2,1)}), bf16[16,4,64,512]{3,2,1,0:T(8,128)(2,1)}) %all-gather.9.cloned.1.call-update) | async-done | bytes 4194320 | tf_op jit(solution)/shard_map/all_gather | solution.py:254
  59.8 5.8 %shard_map.85 = (f32[4,2,4,64,128]{4,3,2,1,0:T(8,128)}, f32[4,1,512]{2,1,0:T(1,128)}) custom-call(f32[16]{0:T(128)} %wr_ref.15, f32[16]{0:T(128)} %wi_ref.15, bf16[8,2,4,64,512]{4,3,2,1,0:T(8,128)(2,1)} %bitcast.21, bf16[16,64,512]{2,1,0:T(8,128)(2,1)} %own_r_ref.15, bf16[16,64,512]{2,1,0:T(8,128)(2,1)} %own_i_ref.15, f32[16,64,512]{2,1,0:T(8,128)} %rest_0_.7, ...), custom_call_target="tpu_custom_call" | custom-call | flops 1073741824 | bytes 6815744 | tf_op jit(solution)/shard_map/pallas_call | solution.py:68
  65.6 2.2 convert_element_type.30
  67.8 3.6 all-to-all-start
  71.3 35.7 %all-gather.11.cloned.1.call-done = bf16[16,4,64,512]{3,2,1,0:T(8,128)(2,1)} async-done(((bf16[2,4,64,512]{3,2,1,0:T(8,128)(2,1)}), bf16[16,4,64,512]{3,2,1,0:T(8,128)(2,1)}) %all-gather.11.cloned.1.call-update) | async-done | bytes 4194320 | tf_op jit(solution)/shard_map/all_gather | solution.py:254
  107.1 5.8 %shard_map.86 = (f32[4,2,4,64,128]{4,3,2,1,0:T(8,128)}, f32[4,1,512]{2,1,0:T(1,128)}) custom-call(f32[16]{0:T(128)} %wr_ref.15, f32[16]{0:T(128)} %wi_ref.15, bf16[8,2,4,64,512]{4,3,2,1,0:T(8,128)(2,1)} %bitcast.23, bf16[16,64,512]{2,1,0:T(8,128)(2,1)} %own_r_ref.15, bf16[16,64,512]{2,1,0:T(8,128)(2,1)} %own_i_ref.15, f32[16,64,512]{2,1,0:T(8,128)} %rest_0_.7, ...), custom_call_target="tpu_custom_call" | custom-call | flops 1073741824 | bytes 6815744 | tf_op jit(solution)/shard_map/pallas_call | solution.py:68
  112.9 2.2 convert_element_type.32
  115.1 3.6 all-to-all-start.1
  118.7 35.7 %all-gather.13.cloned.1.call-done = bf16[16,4,64,512]{3,2,1,0:T(8,128)(2,1)} async-done(((bf16[2,4,64,512]{3,2,1,0:T(8,128)(2,1)}), bf16[16,4,64,512]{3,2,1,0:T(8,128)(2,1)}) %all-gather.13.cloned.1.call-update) | async-done | bytes 4194320 | tf_op jit(solution)/shard_map/all_gather | solution.py:254
  154.4 5.8 %shard_map.87 = (f32[4,2,4,64,128]{4,3,2,1,0:T(8,128)}, f32[4,1,512]{2,1,0:T(1,128)}) custom-call(f32[16]{0:T(128)} %wr_ref.15, f32[16]{0:T(128)} %wi_ref.15, bf16[8,2,4,64,512]{4,3,2,1,0:T(8,128)(2,1)} %bitcast.25, bf16[16,64,512]{2,1,0:T(8,128)(2,1)} %own_r_ref.15, bf16[16,64,512]{2,1,0:T(8,128)(2,1)} %own_i_ref.15, f32[16,64,512]{2,1,0:T(8,128)} %rest_0_.7, ...), custom_call_target="tpu_custom_call" | custom-call | flops 1073741824 | bytes 6815744 | tf_op jit(solution)/shard_map/pallas_call | solution.py:68
  160.2 2.2 convert_element_type.34
  162.4 3.6 all-to-all-start.2
  166.0 35.5 %all-gather.15.cloned.1.call-done = bf16[16,4,64,512]{3,2,1,0:T(8,128)(2,1)} async-done(((bf16[2,4,64,512]{3,2,1,0:T(8,128)(2,1)}), bf16[16,4,64,512]{3,2,1,0:T(8,128)(2,1)}) %all-gather.15.cloned.1.call-update) | async-done | bytes 4194320 | tf_op jit(solution)/shard_map/all_gather | solution.py:254
  201.5 5.8 %shard_map.88 = (f32[4,2,4,64,128]{4,3,2,1,0:T(8,128)}, f32[4,1,512]{2,1,0:T(1,128)}) custom-call(f32[16]{0:T(128)} %wr_ref.15, f32[16]{0:T(128)} %wi_ref.15, bf16[8,2,4,64,512]{4,3,2,1,0:T(8,128)(2,1)} %bitcast.27, bf16[16,64,512]{2,1,0:T(8,128)(2,1)} %own_r_ref.15, bf16[16,64,512]{2,1,0:T(8,128)(2,1)} %own_i_ref.15, f32[16,64,512]{2,1,0:T(8,128)} %rest_0_.7, ...), custom_call_target="tpu_custom_call" | custom-call | flops 1073741824 | bytes 6815744 | tf_op jit(solution)/shard_map/pallas_call | solution.py:68
  207.4 2.1 convert_element_type.36
  209.5 3.6 all-to-all-start.3
  213.2 1.1 convert_element_type.31.refs_0_
  214.2 1.1 convert_element_type.33.refs_1_
  215.3 1.1 convert_element_type.35.refs_2_
  216.3 5.3 %all-to-all-done.3 = f16[4,2,4,64,128]{4,3,2,1,0:T(8,128)(2,1)S(1)} async-done(((f16[4,2,4,64,128]{4,3,2,1,0:T(8,128)(2,1)}), f16[4,2,4,64,128]{4,3,2,1,0:T(8,128)(2,1)S(1)}, u32[]{:S(2)}, u32[]{:S(2)}) %all-to-all-start.3) | async-done | bytes 524320 | tf_op jit(solution)/shard_map/all_to_all | solution.py:243
  221.6 1.1 convert_element_type.37.refs_3_
  222.7 6.6 %shard_map.89 = f32[4,2,16,64,128]{4,3,2,1,0:T(8,128)} custom-call(f32[4,2,4,64,128]{4,3,2,1,0:T(8,128)} %convert_element_type.31.refs_0_, f32[4,2,4,64,128]{4,3,2,1,0:T(8,128)} %convert_element_type.33.refs_1_, f32[4,2,4,64,128]{4,3,2,1,0:T(8,128)} %convert_element_type.35.refs_2_, f32[4,2,4,64,128]{4,3,2,1,0:T(8,128)} %convert_element_type.37.refs_3_), custom_call_target="tpu_custom_call" | custom-call | flops 32768000 | bytes 8388608 | tf_op jit(solution)/shard_map/pallas_call | solution.py:174
  229.4 2.7 convert_element_type.38
  232.1 27.5 %all_to_all.50 = f16[4,2,16,64,128]{4,3,2,1,0:T(8,128)(2,1)S(1)} all-to-all(f16[4,2,16,64,128]{4,3,2,1,0:T(8,128)(2,1)S(1)} %convert_element_type.38), channel_id=1, replica_groups=mesh['af'=4,'sa'=8] {'af'}, dimensions={0} | all-to-all | bytes 4194304 | tf_op jit(solution)/shard_map/all_to_all | solution.py:243
  259.6 2.5 convert_multiply_fusion.rest_0_
  262.1 5.8 %shard_map.93 = (f32[4,2,4,64,128]{4,3,2,1,0:T(8,128)}, f32[4,1,512]{2,1,0:T(1,128)}) custom-call(f32[16]{0:T(128)} %wr_ref.15, f32[16]{0:T(128)} %wi_ref.15, bf16[8,2,4,64,512]{4,3,2,1,0:T(8,128)(2,1)} %bitcast.28, bf16[16,64,512]{2,1,0:T(8,128)(2,1)} %own_r_ref.15, bf16[16,64,512]{2,1,0:T(8,128)(2,1)} %own_i_ref.15, ...), custom_call_target="tpu_custom_call" | custom-call | flops 1073741824 | bytes 6815744 | tf_op jit(solution)/shard_map/pallas_call | solution.py:68
  267.9 3.5 all-to-all-start.8
  271.4 5.9 %shard_map.92 = (f32[4,2,4,64,128]{4,3,2,1,0:T(8,128)}, f32[4,1,512]{2,1,0:T(1,128)}) custom-call(f32[16]{0:T(128)} %wr_ref.15, f32[16]{0:T(128)} %wi_ref.15, bf16[8,2,4,64,512]{4,3,2,1,0:T(8,128)(2,1)} %bitcast.26, bf16[16,64,512]{2,1,0:T(8,128)(2,1)} %own_r_ref.15, bf16[16,64,512]{2,1,0:T(8,128)(2,1)} %own_i_ref.15, ...), custom_call_target="tpu_custom_call" | custom-call | flops 1073741824 | bytes 6815744 | tf_op jit(solution)/shard_map/pallas_call | solution.py:68
  277.3 5.9 %all-to-all-done.8.refs_3_ = f32[4,2,4,64,128]{4,3,2,1,0:T(8,128)S(1)} async-done(((f32[4,2,4,64,128]{4,3,2,1,0:T(8,128)}), f32[4,2,4,64,128]{4,3,2,1,0:T(8,128)S(1)}, u32[]{:S(2)}, u32[]{:S(2)}) %all-to-all-start.8) | async-done | bytes 1048608 | tf_op jit(solution)/shard_map/all_to_all | solution.py:243
  283.1 3.5 all-to-all-start.7
  286.7 5.9 %shard_map.91 = (f32[4,2,4,64,128]{4,3,2,1,0:T(8,128)}, f32[4,1,512]{2,1,0:T(1,128)}) custom-call(f32[16]{0:T(128)} %wr_ref.15, f32[16]{0:T(128)} %wi_ref.15, bf16[8,2,4,64,512]{4,3,2,1,0:T(8,128)(2,1)} %bitcast.24, bf16[16,64,512]{2,1,0:T(8,128)(2,1)} %own_r_ref.15, bf16[16,64,512]{2,1,0:T(8,128)(2,1)} %own_i_ref.15, ...), custom_call_target="tpu_custom_call" | custom-call | flops 1073741824 | bytes 6815744 | tf_op jit(solution)/shard_map/pallas_call | solution.py:68
  292.5 7.2 %all-to-all-done.7.refs_2_ = f32[4,2,4,64,128]{4,3,2,1,0:T(8,128)S(1)} async-done(((f32[4,2,4,64,128]{4,3,2,1,0:T(8,128)}), f32[4,2,4,64,128]{4,3,2,1,0:T(8,128)S(1)}, u32[]{:S(2)}, u32[]{:S(2)}) %all-to-all-start.7) | async-done | bytes 1048608 | tf_op jit(solution)/shard_map/all_to_all | solution.py:243
  299.8 3.5 all-to-all-start.6
  303.3 5.8 %shard_map.90 = (f32[4,2,4,64,128]{4,3,2,1,0:T(8,128)}, f32[4,1,512]{2,1,0:T(1,128)}) custom-call(f32[16]{0:T(128)} %wr_ref.15, f32[16]{0:T(128)} %wi_ref.15, bf16[8,2,4,64,512]{4,3,2,1,0:T(8,128)(2,1)} %bitcast.22, bf16[16,64,512]{2,1,0:T(8,128)(2,1)} %own_r_ref.15, bf16[16,64,512]{2,1,0:T(8,128)(2,1)} %own_i_ref.15, ...), custom_call_target="tpu_custom_call" | custom-call | flops 1073741824 | bytes 6815744 | tf_op jit(solution)/shard_map/pallas_call | solution.py:68
  309.1 7.3 %all-to-all-done.6.refs_1_ = f32[4,2,4,64,128]{4,3,2,1,0:T(8,128)S(1)} async-done(((f32[4,2,4,64,128]{4,3,2,1,0:T(8,128)}), f32[4,2,4,64,128]{4,3,2,1,0:T(8,128)S(1)}, u32[]{:S(2)}, u32[]{:S(2)}) %all-to-all-start.6) | async-done | bytes 1048608 | tf_op jit(solution)/shard_map/all_to_all | solution.py:243
  316.4 18.0 %all_to_all.51.refs_0_ = f32[4,2,4,64,128]{4,3,2,1,0:T(8,128)} all-to-all(f32[4,2,4,64,128]{4,3,2,1,0:T(8,128)} %get-tuple-element.23), channel_id=1, replica_groups=mesh['af'=4,'sa'=8] {'af'}, dimensions={0} | all-to-all | bytes 2097152 | tf_op jit(solution)/shard_map/all_to_all | solution.py:243
  334.4 6.6 %shard_map.94 = f32[4,2,16,64,128]{4,3,2,1,0:T(8,128)} custom-call(f32[4,2,4,64,128]{4,3,2,1,0:T(8,128)} %all_to_all.51.refs_0_, f32[4,2,4,64,128]{4,3,2,1,0:T(8,128)} %copy-done.2, f32[4,2,4,64,128]{4,3,2,1,0:T(8,128)} %copy-done.1, f32[4,2,4,64,128]{4,3,2,1,0:T(8,128)} %copy-done), custom_call_target="tpu_custom_call" | custom-call | flops 32768000 | bytes 8388608 | tf_op jit(solution)/shard_map/pallas_call | solution.py:174
  341.1 5.2 %all-to-all-start.9 = ((f32[4,2,16,64,128]{4,3,2,1,0:T(8,128)}), f32[4,2,16,64,128]{4,3,2,1,0:T(8,128)}, u32[]{:S(2)}, u32[]{:S(2)}) async-start(f32[4,2,16,64,128]{4,3,2,1,0:T(8,128)} %shard_map.94), calls=%async_computation.9 | async-start | bytes 8388608 | tf_op jit(solution)/shard_map/all_to_all | solution.py:243
  346.3 0.6 reduce_sum.46
  346.9 0.6 reduce_sum.47
  347.5 0.6 reduce_sum.52
  348.1 0.6 reduce_sum.54
  351.3 0.6 reduce_sum.56
  351.9 0.6 reduce_sum.60
  352.5 0.6 reduce_sum.76
  353.1 0.6 reduce_sum.78
  356.3 0.7 broadcast_select_fusion.own_ref
  356.9 38.1 %shard_map.95 = f32[8,128]{1,0:T(8,128)} custom-call(f32[8,128]{1,0:T(8,128)} %broadcast_select_fusion.own_ref), custom_call_target="tpu_custom_call" | custom-call | tf_op jit(solution)/shard_map/pallas_call | solution.py:228
  395.0 1.3 multiply_reduce_fusion
  396.3 4.0 fusion
  400.3 1.4 copy.12
  401.7 1.8 squeeze.8
  403.6 3.0 copy.11
  406.6 1.8 squeeze.7
  (31 shorter events, 0.1 us)
Async XLA Ops:
  7.2 52.6 %all-gather.9.cloned.1.call-start = ((), (), s32[]{:S(2)}) async-start(), calls=%async_computation.10 | async-start | bytes 4718592 | tf_op jit(solution)/shard_map/all_gather | solution.py:254
  9.7 97.3 %all-gather.11.cloned.1.call-start = ((), (), s32[]{:S(2)}) async-start(), calls=%async_computation.11 | async-start | bytes 4718592 | tf_op jit(solution)/shard_map/all_gather | solution.py:254
  10.7 143.7 %all-gather.13.cloned.1.call-start = ((), (), s32[]{:S(2)}) async-start(), calls=%async_computation.12 | async-start | bytes 4718592 | tf_op jit(solution)/shard_map/all_gather | solution.py:254
  11.6 190.0 %all-gather.15.cloned.1.call-start = ((), (), s32[]{:S(2)}) async-start(), calls=%async_computation.13 | async-start | bytes 4718592 | tf_op jit(solution)/shard_map/all_gather | solution.py:254
  67.8 47.3 %all-to-all-start = ((f16[4,2,4,64,128]{4,3,2,1,0:T(8,128)(2,1)}), f16[4,2,4,64,128]{4,3,2,1,0:T(8,128)(2,1)S(1)}, u32[]{:S(2)}, u32[]{:S(2)}) async-start(f16[4,2,4,64,128]{4,3,2,1,0:T(8,128)(2,1)} %convert_element_type.30), calls=%async_computation | async-start | bytes 1048576 | tf_op jit(solution)/shard_map/all_to_all | solution.py:243
  115.1 47.3 %all-to-all-start.1 = ((f16[4,2,4,64,128]{4,3,2,1,0:T(8,128)(2,1)}), f16[4,2,4,64,128]{4,3,2,1,0:T(8,128)(2,1)S(1)}, u32[]{:S(2)}, u32[]{:S(2)}) async-start(f16[4,2,4,64,128]{4,3,2,1,0:T(8,128)(2,1)} %convert_element_type.32), calls=%async_computation.1 | async-start | bytes 1048576 | tf_op jit(solution)/shard_map/all_to_all | solution.py:243
  162.4 47.1 %all-to-all-start.2 = ((f16[4,2,4,64,128]{4,3,2,1,0:T(8,128)(2,1)}), f16[4,2,4,64,128]{4,3,2,1,0:T(8,128)(2,1)S(1)}, u32[]{:S(2)}, u32[]{:S(2)}) async-start(f16[4,2,4,64,128]{4,3,2,1,0:T(8,128)(2,1)} %convert_element_type.34), calls=%async_computation.2 | async-start | bytes 1048576 | tf_op jit(solution)/shard_map/all_to_all | solution.py:243
  209.5 12.1 %all-to-all-start.3 = ((f16[4,2,4,64,128]{4,3,2,1,0:T(8,128)(2,1)}), f16[4,2,4,64,128]{4,3,2,1,0:T(8,128)(2,1)S(1)}, u32[]{:S(2)}, u32[]{:S(2)}) async-start(f16[4,2,4,64,128]{4,3,2,1,0:T(8,128)(2,1)} %convert_element_type.36), calls=%async_computation.3 | async-start | bytes 1048576 | tf_op jit(solution)/shard_map/all_to_all | solution.py:243
  267.9 15.3 %all-to-all-start.8 = ((f32[4,2,4,64,128]{4,3,2,1,0:T(8,128)}), f32[4,2,4,64,128]{4,3,2,1,0:T(8,128)S(1)}, u32[]{:S(2)}, u32[]{:S(2)}) async-start(f32[4,2,4,64,128]{4,3,2,1,0:T(8,128)} %get-tuple-element.26), calls=%async_computation.8 | async-start | bytes 2097152 | tf_op jit(solution)/shard_map/all_to_all | solution.py:243
  283.1 9.4 %copy-start = (f32[4,2,4,64,128]{4,3,2,1,0:T(8,128)}, f32[4,2,4,64,128]{4,3,2,1,0:T(8,128)S(1)}, u32[]{:S(2)}) copy-start(f32[4,2,4,64,128]{4,3,2,1,0:T(8,128)S(1)} %all-to-all-done.8.refs_3_) | copy-start | bytes 3145732
  283.1 16.6 %all-to-all-start.7 = ((f32[4,2,4,64,128]{4,3,2,1,0:T(8,128)}), f32[4,2,4,64,128]{4,3,2,1,0:T(8,128)S(1)}, u32[]{:S(2)}, u32[]{:S(2)}) async-start(f32[4,2,4,64,128]{4,3,2,1,0:T(8,128)} %get-tuple-element.25), calls=%async_computation.7 | async-start | bytes 2097152 | tf_op jit(solution)/shard_map/all_to_all | solution.py:243
  299.8 9.4 %copy-start.1 = (f32[4,2,4,64,128]{4,3,2,1,0:T(8,128)}, f32[4,2,4,64,128]{4,3,2,1,0:T(8,128)S(1)}, u32[]{:S(2)}) copy-start(f32[4,2,4,64,128]{4,3,2,1,0:T(8,128)S(1)} %all-to-all-done.7.refs_2_) | copy-start | bytes 3145732
  299.8 16.6 %all-to-all-start.6 = ((f32[4,2,4,64,128]{4,3,2,1,0:T(8,128)}), f32[4,2,4,64,128]{4,3,2,1,0:T(8,128)S(1)}, u32[]{:S(2)}, u32[]{:S(2)}) async-start(f32[4,2,4,64,128]{4,3,2,1,0:T(8,128)} %get-tuple-element.24), calls=%async_computation.6 | async-start | bytes 2097152 | tf_op jit(solution)/shard_map/all_to_all | solution.py:243
  316.4 18.0 %copy-start.2 = (f32[4,2,4,64,128]{4,3,2,1,0:T(8,128)}, f32[4,2,4,64,128]{4,3,2,1,0:T(8,128)S(1)}, u32[]{:S(2)}) copy-start(f32[4,2,4,64,128]{4,3,2,1,0:T(8,128)S(1)} %all-to-all-done.6.refs_1_) | copy-start | bytes 3145732
  341.0 5.3 %copy-start.3 = (f32[4,1,512]{2,1,0:T(1,128)S(1)}, f32[4,1,512]{2,1,0:T(1,128)}, u32[]{:S(2)}) copy-start(f32[4,1,512]{2,1,0:T(1,128)} %get-tuple-element.27) | copy-start | bytes 24580
  341.0 5.9 %copy-start.4 = (f32[4,1,512]{2,1,0:T(1,128)S(1)}, f32[4,1,512]{2,1,0:T(1,128)}, u32[]{:S(2)}) copy-start(f32[4,1,512]{2,1,0:T(1,128)} %get-tuple-element.28) | copy-start | bytes 24580
  341.0 6.5 %copy-start.5 = (f32[4,1,512]{2,1,0:T(1,128)S(1)}, f32[4,1,512]{2,1,0:T(1,128)}, u32[]{:S(2)}) copy-start(f32[4,1,512]{2,1,0:T(1,128)} %get-tuple-element.29) | copy-start | bytes 24580
  341.0 7.1 %copy-start.6 = (f32[4,1,512]{2,1,0:T(1,128)S(1)}, f32[4,1,512]{2,1,0:T(1,128)}, u32[]{:S(2)}) copy-start(f32[4,1,512]{2,1,0:T(1,128)} %get-tuple-element.30) | copy-start | bytes 24580
  341.0 10.2 %copy-start.10 = (f32[4,1,512]{2,1,0:T(1,128)S(1)}, f32[4,1,512]{2,1,0:T(1,128)}, u32[]{:S(2)}) copy-start(f32[4,1,512]{2,1,0:T(1,128)} %get-tuple-element.31) | copy-start | bytes 24580
  341.0 10.8 %copy-start.9 = (f32[4,1,512]{2,1,0:T(1,128)S(1)}, f32[4,1,512]{2,1,0:T(1,128)}, u32[]{:S(2)}) copy-start(f32[4,1,512]{2,1,0:T(1,128)} %get-tuple-element.32) | copy-start | bytes 24580
  341.1 11.5 %copy-start.8 = (f32[4,1,512]{2,1,0:T(1,128)S(1)}, f32[4,1,512]{2,1,0:T(1,128)}, u32[]{:S(2)}) copy-start(f32[4,1,512]{2,1,0:T(1,128)} %get-tuple-element.33) | copy-start | bytes 24580
  341.1 12.1 %copy-start.7 = (f32[4,1,512]{2,1,0:T(1,128)S(1)}, f32[4,1,512]{2,1,0:T(1,128)}, u32[]{:S(2)}) copy-start(f32[4,1,512]{2,1,0:T(1,128)} %get-tuple-element.34) | copy-start | bytes 24580
  341.1 55.2 %all-to-all-start.9 = ((f32[4,2,16,64,128]{4,3,2,1,0:T(8,128)}), f32[4,2,16,64,128]{4,3,2,1,0:T(8,128)}, u32[]{:S(2)}, u32[]{:S(2)}) async-start(f32[4,2,16,64,128]{4,3,2,1,0:T(8,128)} %shard_map.94), calls=%async_computation.9 | async-start | bytes 8388608 | tf_op jit(solution)/shard_map/all_to_all | solution.py:243
Sparse Core Ops, SparseCore 0:
  10.1 49.5 all-gather.8
  61.4 45.6 all-gather.10
  108.7 45.6 all-gather.12
  155.8 45.6 all-gather.14

commit v2 on v1

--- a/solution.py
+++ b/solution.py
@@ -11,7 +11,9 @@
 ITERS = 2
 STEP_LENGTH = 0.02
 THRESHOLD = 0.25
-CHUNKS = 4
+CHUNKS = 2
+WIRE = jnp.float16
+LARGEST = 60000.0
 GROUP = 8
 HALF = math.sqrt(0.5)
 MESH = pl.DeviceIdType.MESH
@@ -23,10 +25,10 @@
         gr = gr_ref[0]
         gi = gi_ref[0]
     else:
-        g_ref, out_ref, sum_ref = rest
+        g_ref, gi_ref, out_ref, sum_ref = rest
         parts = g_ref.shape[0]
-        gr = jnp.concatenate([g_ref[a, 0, 0] for a in range(parts)], axis=1)
-        gi = jnp.concatenate([g_ref[a, 1, 0] for a in range(parts)], axis=1)
+        gr = jnp.concatenate([g_ref[a, 0] for a in range(parts)], axis=1)
+        gi = jnp.concatenate([gi_ref[a, 0] for a in range(parts)], axis=1)
     at = pl.program_id(0) + offset
     qr = wr_ref[at]
     qi = wi_ref[at]
@@ -55,7 +57,7 @@
         out_ref[a, 1, 0] = zi[:, a * width : (a + 1) * width]
 
 
-def product(offset, count, parts, wr, wi, whole, own_r, own_i, current):
+def product(offset, count, local, parts, wr, wi, whole, own_r, own_i, current):
     sa, _, _, rows, n = whole.shape
     first = len(current) == 2
     plain = pl.BlockSpec((1, rows, n), lambda f: (f + offset, 0, 0))
@@ -64,7 +66,12 @@
     if first:
         cur_specs = [plain, plain]
     else:
-        cur_specs = [pl.BlockSpec((parts, 2, 1, rows, width), lambda f: (0, 0, f + offset, 0, 0))]
+        block = (parts, 1, rows, width)
+        cur_specs = [
+            pl.BlockSpec(block, lambda f: (0, f + offset, 0, 0)),
+            pl.BlockSpec(block, lambda f: (0, f + offset + local, 0, 0)),
+        ]
+        current = (current[0], current[0])
     return pl.pallas_call(
         functools.partial(product_kernel, first, offset),
         grid=(count,),
@@ -120,12 +127,14 @@
     return v - jnp.clip(v, -THRESHOLD, THRESHOLD)
 
 
-def transform_kernel(pieces, in_scale, out_scale, *refs):
-    in_refs, out_ref, work = refs[:pieces], refs[pieces], refs[pieces + 1]
-    parts, _, local, block, width = out_ref.shape
+def transform_kernel(pieces, bound, *refs):
+    scale_ref, in_refs, out_ref, work = refs[0], refs[1 : pieces + 1], refs[pieces + 1], refs[pieces + 2]
+    parts, slots, block, width = out_ref.shape
+    local = slots // 2
     piece = local // pieces
     radix = 8
-    factor = 1.0 / radix
+    in_scale = scale_ref[0] / radix
+    out_scale = scale_ref[1] / radix
 
     def one(g, _):
         at = pl.ds(pl.multiple_of(g * GROUP, GROUP), GROUP)
@@ -134,10 +143,9 @@
             a, b = divmod(f, local)
             c, d = divmod(b, piece)
             ref = in_refs[c]
-            scale = factor * in_scale
             return (
-                ref[a, 0, d, at, :].astype(jnp.float32) * scale,
-                ref[a, 1, d, at, :].astype(jnp.float32) * scale,
+                ref[a, 0, d, at, :].astype(jnp.float32) * in_scale,
+                ref[a, 1, d, at, :].astype(jnp.float32) * in_scale,
             )
 
         for f1 in range(radix):
@@ -154,35 +162,44 @@
                 v = rotate(y[f1], -f1 * t2 / 64) if f1 * t2 else y[f1]
                 work[0, radix * f1 + t2] = v[0]
                 work[1, radix * f1 + t2] = v[1]
+        largest = jnp.zeros((GROUP, width), jnp.float32)
         for f1 in range(radix):
             y = eight([(work[0, radix * f1 + t2], work[1, radix * f1 + t2]) for t2 in range(radix)], -1)
             for f2 in range(radix):
                 a, b = divmod(f1 + radix * f2, local)
-                scale = factor * out_scale
-                out_ref[a, 0, b, at, :] = y[f2][0] * scale
-                out_ref[a, 1, b, at, :] = y[f2][1] * scale
+                re, im = y[f2][0] * out_scale, y[f2][1] * out_scale
+                out_ref[a, b, at, :] = re
+                out_ref[a, b + local, at, :] = im
+                if bound:
+                    largest = jnp.maximum(largest, jnp.maximum(jnp.abs(re), jnp.abs(im)))
+        if bound:
+            for a in range(parts):
+                out_ref[a, 2 * local, at, :] = largest
         return 0
 
     lax.fori_loop(0, block // GROUP, one, 0)
 
 
-def transform(arrays, in_scale, out_scale):
+def transform(arrays, in_scale, out_scale, bound):
     pieces = len(arrays)
     parts, _, piece, rows, width = arrays[0].shape
     local = piece * pieces
     block = min(16, rows)
+    slots = 2 * local + (1 if bound else 0)
+    scales = jnp.stack([jnp.float32(in_scale), jnp.float32(out_scale)])
     return pl.pallas_call(
-        functools.partial(transform_kernel, pieces, in_scale, out_scale),
+        functools.partial(transform_kernel, pieces, bound),
         grid=(rows // block,),
-        in_specs=[pl.BlockSpec((parts, 2, piece, block, width), lambda r: (0, 0, 0, r, 0))] * pieces,
-        out_specs=pl.BlockSpec((parts, 2, local, block, width), lambda r: (0, 0, 0, r, 0)),
-        out_shape=jax.ShapeDtypeStruct((parts, 2, local, rows, width), jnp.float32),
+        in_specs=[pl.BlockSpec(memory_space=pltpu.SMEM)]
+        + [pl.BlockSpec((parts, 2, piece, block, width), lambda r: (0, 0, 0, r, 0))] * pieces,
+        out_specs=pl.BlockSpec((parts, slots, block, width), lambda r: (0, 0, r, 0)),
+        out_shape=jax.ShapeDtypeStruct((parts, slots, rows, width), jnp.float32),
         scratch_shapes=[pltpu.VMEM((2, parts * local, GROUP, width), jnp.float32)],
         cost_estimate=pl.CostEstimate(
             flops=4000 * rows * width, bytes_accessed=16 * parts * local * rows * width, transcendentals=0
         ),
         compiler_params=pltpu.CompilerParams(vmem_limit_bytes=60 * 2**20),
-    )(*arrays)
+    )(scales, *arrays)
 
 
 def total_kernel(counts, own_ref, out_ref, slots, send_sem, recv_sem):
@@ -243,39 +260,80 @@
     return lax.all_to_all(values, "af", split_axis=0, concat_axis=0, tiled=True)
 
 
+def join_kernel(scale_ref, re_ref, im_ref, out_re, out_im):
+    parts, _, _, width = re_ref.shape
+    scale = scale_ref[0]
+    for a in range(parts):
+        cut = slice(a * width, (a + 1) * width)
+        out_re[:, :, cut] = re_ref[a] * scale
+        out_im[:, :, cut] = im_ref[a] * scale
+
+
+def join(current, scale, local):
+    parts, _, rows, width = current.shape
+    count = max(1, local // 4)
+    out = jax.ShapeDtypeStruct((local, rows, parts * width), jnp.float32)
+    out_spec = pl.BlockSpec((count, rows, parts * width), lambda f: (f, 0, 0))
+    block = (parts, count, rows, width)
+    steps = local // count
+    return pl.pallas_call(
+        join_kernel,
+        grid=(steps,),
+        in_specs=[
+            pl.BlockSpec(memory_space=pltpu.SMEM),
+            pl.BlockSpec(block, lambda f: (0, f, 0, 0)),
+            pl.BlockSpec(block, lambda f: (0, f + steps, 0, 0)),
+        ],
+        out_specs=[out_spec, out_spec],
+        out_shape=[out, out],
+        compiler_params=pltpu.CompilerParams(vmem_limit_bytes=60 * 2**20),
+    )(scale.reshape(1), current, current)
+
+
 def on_device(counts, data_real, data_imaginary, wave_real, wave_imaginary, primaries_real, primaries_imaginary):
     parts = counts[0]
     local, rows, n = data_real.shape
+    freqs = local * parts
     size = local // CHUNKS
     wholes = []
     for c in range(CHUNKS):
         cut = slice(c * size, (c + 1) * size)
         both = jnp.stack([data_real[cut], data_imaginary[cut]])
         wholes.append(lax.all_gather(both, "sa", axis=0))
-    first = (primaries_real, primaries_imaginary)
+    gain = 1.01 * (2 * 2.5 + n)
+    spread = 1.01 * math.sqrt(2 * freqs)
+
+    def stepped_bound(g):
+        return g + STEP_LENGTH * gain * (0.5 + gain * g)
+
+    z_scale = 1.0
+    z_bound = stepped_bound(3.0)
     sums = []
-    current = None
+    current = (primaries_real, primaries_imaginary)
     for iteration in range(ITERS):
-        wire = jnp.float16 if iteration == 0 else jnp.float32
-        traces = []
+        last = iteration == ITERS - 1
+        traces = [None] * CHUNKS
         squares = []
         for c in range(CHUNKS):
             stepped, square = product(
-                c * size, size, parts, wave_real, wave_imaginary, wholes[c], data_real, data_imaginary,
-                first if iteration == 0 else (current,),
+                c * size, size, local, parts, wave_real, wave_imaginary, wholes[c], data_real, data_imaginary, current,
             )
             squares.append(square)
-            traces.append(exchange(stepped.astype(wire)).astype(jnp.float32))
+            traces[c] = exchange((stepped * (1.0 / z_scale)).astype(WIRE)).astype(jnp.float32)
         sums.append(jnp.sum(jnp.concatenate(squares)))
-        scale = 0.25 if iteration == 0 else 1.0
-        back = transform(traces, 1.0, scale)
-        current = exchange(back.astype(wire)).astype(jnp.float32)
-        if iteration == 0:
-            current = current / scale
-    updated = current.transpose(1, 2, 3, 0, 4).reshape(2, local, rows, n)
+        g_scale = spread * z_bound / LARGEST
+        back = transform(traces, z_scale, 1.0 / g_scale, not last)
+        moved = exchange(back.astype(WIRE)).astype(jnp.float32)
+        if last:
+            updated = join(moved, jnp.float32(g_scale), local)
+        else:
+            g_bound = 1.002 * g_scale * jnp.max(moved[:, 2 * local]) + 1e-6
+            current = (moved * g_scale,)
+            z_bound = stepped_bound(g_bound)
+            z_scale = z_bound / LARGEST
     row = lax.broadcasted_iota(jnp.int32, (8, 128), 0)
     own = jnp.where(row == 0, sums[0], jnp.where(row == 1, sums[1], 0.0))
-    misfit = total(own, counts)[:ITERS, 0] / (parts * local * n * n)
+    misfit = total(own, counts)[:ITERS, 0] / (freqs * n * n)
     return (updated[0], updated[1], misfit)
 
 

time: 417 us -> 359 us (0.86)
  blocking collectives: 45.4 us -> 28.4 us
  Pallas kernels: 98 us -> 81.9 us
  local copies, waits for them, and re-layouts: 13.8 us -> 1.68 us
  starting transfers between devices: 30.3 us -> 18.8 us
  other arithmetic: 28.5 us -> 37.9 us
  waiting for transfers between devices: 180 us -> 171 us
    all_to_all x2 -> x1, blocking collectives: 45.4 us -> 28.4 us  [exchange(): return lax.all_to_all(values, 'af', split_axis=0, concat_axis=0, tiled=True)]
    pallas_call x1, Pallas kernels: 38.1 us -> 22 us  [total(): pl.pallas_call(functools.partial(total_kernel, counts), out_shape=jax.Sha...]
    convert_element_type x9 -> x12, other arithmetic: 15.7 us -> 27.4 us  [the longest x4 11.5 us: on_device(): (stepped * (1.0 / z_scale)).astype(WIRE)]
    all_to_all x8 -> x5, starting transfers between devices: 30.2 us -> 18.8 us  [exchange(): return lax.all_to_all(values, 'af', split_axis=0, concat_axis=0, tiled=True)]
    slice x3 -> x0, local copies, waits for them, and re-layouts: 8.38 us -> none  [on_device(): return (updated[0], updated[1], misfit)]
    pallas_call x8 -> x4, Pallas kernels: 46.6 us -> 41.6 us  [product(): pl.pallas_call(functools.partial(product_kernel, first, offset), grid=(co...]
    pallas_call x2 -> x3, Pallas kernels: 13.3 us -> 18.3 us  [the longest x2 13.5 us: transform(): pl.pallas_call(functools.partial(transform_kernel, pieces, bound), grid=(...]
    all_gather x4 -> x2, waiting for transfers between devices: 154 us -> 149 us  [on_device(): wholes.append(lax.all_gather(both, 'sa', axis=0))]
  transfers between devices with their start and end apart: 12 -> 7, of which waited for: 8 -> 4; matrix products, arithmetic and copies ran while one was open for 5% -> 5% of each run, Pallas kernels for 19% -> 15%
where the time goes in v2:
time: 359 us; the launch traced here: 358 us
  waiting for transfers between devices  171 us (48%)
  Pallas kernels  81.9 us (23%)
  other arithmetic  37.9 us (11%)
  blocking collectives  28.4 us (8%)
  starting transfers between devices  18.8 us (5%)
  between operations  17.5 us (5%)
    all_gather x2, waiting for transfers between devices, on_device(): wholes.append(lax.all_gather(both, 'sa', axis=0))  149 us
    pallas_call x4, Pallas kernels, product(): pl.pallas_call(functools.partial(product_kernel, first, offset), grid=(co...  41.6 us
    all_to_all x1, blocking collectives, exchange(): return lax.all_to_all(values, 'af', split_axis=0, concat_axis=0, tiled=True)  28.4 us
    pallas_call x1, Pallas kernels, total(): pl.pallas_call(functools.partial(total_kernel, counts), out_shape=jax.Sha...  22 us
    all_to_all x5, waiting for transfers between devices, exchange(): return lax.all_to_all(values, 'af', split_axis=0, concat_axis=0, tiled=True)  21.9 us
    all_to_all x5, starting transfers between devices, exchange(): return lax.all_to_all(values, 'af', split_axis=0, concat_axis=0, tiled=True)  18.8 us
    pallas_call x2, Pallas kernels, transform(): pl.pallas_call(functools.partial(transform_kernel, pieces, bound), grid=(...  13.5 us
    convert_element_type x4, other arithmetic, on_device(): (stepped * (1.0 / z_scale)).astype(WIRE)  11.5 us
  transfers between devices with their start and end apart: 7, of which 4 were waited for; matrix products, arithmetic and copies ran while one was open for 5% of the time, Pallas kernels for 15%

profile of v2, /device:TPU:0, one launch (start us, length us, event | category | flops | bytes accessed | tf_op | source)
XLA Modules:
  0.0 357.5 jit_solution(11176112081411550915)
XLA Ops:
  7.2 0.0 all-gather.7.cloned.1.call-start
  7.2 1.7 slice_bitcast_fusion
  8.9 1.1 pad_maximum_fusion.1
  9.9 0.0 all-gather.7.cloned.1.call-update
  10.0 0.0 all-gather.5.cloned.1.call-start
  10.0 1.1 pad_maximum_fusion
  11.1 0.0 all-gather.5.cloned.1.call-update
  11.1 83.8 %all-gather.7.cloned.1.call-done = bf16[16,8,64,512]{3,2,1,0:T(8,128)(2,1)} async-done(((bf16[2,8,64,512]{3,2,1,0:T(8,128)(2,1)}), bf16[16,8,64,512]{3,2,1,0:T(8,128)(2,1)}) %all-gather.7.cloned.1.call-update) | async-done | bytes 8388624 | tf_op jit(solution)/shard_map/all_gather | solution.py:302
  94.9 10.5 %shard_map.86 = (f32[4,2,8,64,128]{4,3,2,1,0:T(8,128)}, f32[8,1,512]{2,1,0:T(1,128)}) custom-call(f32[16]{0:T(128)} %wr_ref.7, f32[16]{0:T(128)} %wi_ref.7, bf16[8,2,8,64,512]{4,3,2,1,0:T(8,128)(2,1)} %bitcast.13, bf16[16,64,512]{2,1,0:T(8,128)(2,1)} %own_r_ref.7, bf16[16,64,512]{2,1,0:T(8,128)(2,1)} %own_i_ref.7, f32[16,64,512]{2,1,0:T(8,128)} %rest_0_.3, ...), custom_call_target="tpu_custom_call" | custom-call | flops 2147483648 | bytes 13631488 | tf_op jit(solution)/shard_map/pallas_call | solution.py:75
  105.4 2.9 convert_element_type.38
  108.3 3.7 %all-to-all-start.1 = ((f16[4,2,8,64,128]{4,3,2,1,0:T(8,128)(2,1)}), f16[4,2,8,64,128]{4,3,2,1,0:T(8,128)(2,1)S(1)}, u32[]{:S(2)}, u32[]{:S(2)}) async-start(f16[4,2,8,64,128]{4,3,2,1,0:T(8,128)(2,1)} %convert_element_type.38), calls=%async_computation.1 | async-start | bytes 2097152 | tf_op jit(solution)/shard_map/all_to_all | solution.py:260
  112.0 65.6 %all-gather.5.cloned.1.call-done = bf16[16,8,64,512]{3,2,1,0:T(8,128)(2,1)} async-done(((bf16[2,8,64,512]{3,2,1,0:T(8,128)(2,1)}), bf16[16,8,64,512]{3,2,1,0:T(8,128)(2,1)}) %all-gather.5.cloned.1.call-update) | async-done | bytes 8388624 | tf_op jit(solution)/shard_map/all_gather | solution.py:302
  177.7 10.3 %shard_map.85 = (f32[4,2,8,64,128]{4,3,2,1,0:T(8,128)}, f32[8,1,512]{2,1,0:T(1,128)}) custom-call(f32[16]{0:T(128)} %wr_ref.7, f32[16]{0:T(128)} %wi_ref.7, bf16[8,2,8,64,512]{4,3,2,1,0:T(8,128)(2,1)} %bitcast.15, bf16[16,64,512]{2,1,0:T(8,128)(2,1)} %own_r_ref.7, bf16[16,64,512]{2,1,0:T(8,128)(2,1)} %own_i_ref.7, f32[16,64,512]{2,1,0:T(8,128)} %rest_0_.3, ...), custom_call_target="tpu_custom_call" | custom-call | flops 2147483648 | bytes 13631488 | tf_op jit(solution)/shard_map/pallas_call | solution.py:75
  188.0 2.9 convert_element_type.36
  190.9 0.0 all-to-all-done.1
  190.9 3.6 %all-to-all-start = ((f16[4,2,8,64,128]{4,3,2,1,0:T(8,128)(2,1)}), f16[4,2,8,64,128]{4,3,2,1,0:T(8,128)(2,1)S(1)}, u32[]{:S(2)}, u32[]{:S(2)}) async-start(f16[4,2,8,64,128]{4,3,2,1,0:T(8,128)(2,1)} %convert_element_type.36), calls=%async_computation | async-start | bytes 2097152 | tf_op jit(solution)/shard_map/all_to_all | solution.py:260
  194.5 1.5 convert_element_type.39.refs_2_
  196.0 12.6 %all-to-all-done = f16[4,2,8,64,128]{4,3,2,1,0:T(8,128)(2,1)S(1)} async-done(((f16[4,2,8,64,128]{4,3,2,1,0:T(8,128)(2,1)}), f16[4,2,8,64,128]{4,3,2,1,0:T(8,128)(2,1)S(1)}, u32[]{:S(2)}, u32[]{:S(2)}) %all-to-all-start) | async-done | bytes 1048608 | tf_op jit(solution)/shard_map/all_to_all | solution.py:260
  208.7 1.5 convert_element_type.37.refs_1_
  210.2 6.8 %shard_map.87 = f32[4,33,64,128]{3,2,1,0:T(8,128)} custom-call(f32[2]{0:T(128)} %constant.4.clone.1.refs_0_, f32[4,2,8,64,128]{4,3,2,1,0:T(8,128)} %convert_element_type.37.refs_1_, f32[4,2,8,64,128]{4,3,2,1,0:T(8,128)} %convert_element_type.39.refs_2_), custom_call_target="tpu_custom_call" | custom-call | flops 32768000 | bytes 8388608 | tf_op jit(solution)/shard_map/pallas_call | solution.py:190
  216.9 2.8 convert_element_type.40
  219.8 28.4 %all_to_all.30 = f16[4,33,64,128]{3,2,1,0:T(8,128)(2,1)S(1)} all-to-all(f16[4,33,64,128]{3,2,1,0:T(8,128)(2,1)S(1)} %convert_element_type.40), channel_id=1, replica_groups=mesh['af'=4,'sa'=8] {'af'}, dimensions={0} | all-to-all | bytes 4325376 | tf_op jit(solution)/shard_map/all_to_all | solution.py:260
  248.1 0.5 convert_element_type.41
  248.6 0.6 slice_reduce_fusion
  249.9 2.6 broadcast_multiply_fusion.rest_0_.rest_1_
  252.5 10.4 %shard_map.89 = (f32[4,2,8,64,128]{4,3,2,1,0:T(8,128)}, f32[8,1,512]{2,1,0:T(1,128)}) custom-call(f32[16]{0:T(128)} %wr_ref.7, f32[16]{0:T(128)} %wi_ref.7, bf16[8,2,8,64,512]{4,3,2,1,0:T(8,128)(2,1)} %bitcast.14, bf16[16,64,512]{2,1,0:T(8,128)(2,1)} %own_r_ref.7, bf16[16,64,512]{2,1,0:T(8,128)(2,1)} %own_i_ref.7, ...), custom_call_target="tpu_custom_call" | custom-call | flops 2147483648 | bytes 13631488 | tf_op jit(solution)/shard_map/pallas_call | solution.py:75
  263.0 2.9 multiply_convert_fusion
  265.8 3.5 all-to-all-start.4
  269.4 10.4 %shard_map.88 = (f32[4,2,8,64,128]{4,3,2,1,0:T(8,128)}, f32[8,1,512]{2,1,0:T(1,128)}) custom-call(f32[16]{0:T(128)} %wr_ref.7, f32[16]{0:T(128)} %wi_ref.7, bf16[8,2,8,64,512]{4,3,2,1,0:T(8,128)(2,1)} %bitcast.16, bf16[16,64,512]{2,1,0:T(8,128)(2,1)} %own_r_ref.7, bf16[16,64,512]{2,1,0:T(8,128)(2,1)} %own_i_ref.7, ...), custom_call_target="tpu_custom_call" | custom-call | flops 2147483648 | bytes 13631488 | tf_op jit(solution)/shard_map/pallas_call | solution.py:75
  279.8 2.9 multiply_convert_fusion.1
  282.6 0.0 all-to-all-done.4
  282.6 4.1 %all-to-all-start.3 = ((f16[4,2,8,64,128]{4,3,2,1,0:T(8,128)(2,1)}), f16[4,2,8,64,128]{4,3,2,1,0:T(8,128)(2,1)S(1)}, u32[]{:S(2)}, u32[]{:S(2)}) async-start(f16[4,2,8,64,128]{4,3,2,1,0:T(8,128)(2,1)} %multiply_convert_fusion.1), calls=%async_computation.3 | async-start | bytes 2097152 | tf_op jit(solution)/shard_map/all_to_all | solution.py:260
  286.8 0.6 pad_maximum_fusion.2.refs_0_
  287.4 1.5 convert_element_type.45.refs_2_
  288.9 9.3 %all-to-all-done.3 = f16[4,2,8,64,128]{4,3,2,1,0:T(8,128)(2,1)S(1)} async-done(((f16[4,2,8,64,128]{4,3,2,1,0:T(8,128)(2,1)}), f16[4,2,8,64,128]{4,3,2,1,0:T(8,128)(2,1)S(1)}, u32[]{:S(2)}, u32[]{:S(2)}) %all-to-all-start.3) | async-done | bytes 1048608 | tf_op jit(solution)/shard_map/all_to_all | solution.py:260
  298.2 1.5 convert_element_type.43.refs_1_
  299.7 6.7 %shard_map.90 = f32[4,32,64,128]{3,2,1,0:T(8,128)} custom-call(f32[2]{0:T(128)} %pad_maximum_fusion.2.refs_0_, f32[4,2,8,64,128]{4,3,2,1,0:T(8,128)} %convert_element_type.43.refs_1_, f32[4,2,8,64,128]{4,3,2,1,0:T(8,128)} %convert_element_type.45.refs_2_), custom_call_target="tpu_custom_call" | custom-call | flops 32768000 | bytes 8388608 | tf_op jit(solution)/shard_map/pallas_call | solution.py:190
  306.4 4.1 %convert_element_type.46 = f16[4,32,64,128]{3,2,1,0:T(8,128)(2,1)} convert(f32[4,32,64,128]{3,2,1,0:T(8,128)} %shard_map.90) | non-fusion elementwise | flops 1048576 | bytes 6291456 | tf_op jit(solution)/shard_map/convert_element_type | solution.py:326
  310.5 0.0 copy-start
  310.5 0.0 copy-start.1
  310.5 0.0 copy-start.2
  310.5 0.0 copy-start.3
  310.5 3.8 %all-to-all-start.5 = ((f16[4,32,64,128]{3,2,1,0:T(8,128)(2,1)}), f16[4,32,64,128]{3,2,1,0:T(8,128)(2,1)S(1)}, u32[]{:S(2)}, u32[]{:S(2)}) async-start(f16[4,32,64,128]{3,2,1,0:T(8,128)(2,1)} %convert_element_type.46), calls=%async_computation.5 | async-start | bytes 4194304 | tf_op jit(solution)/shard_map/all_to_all | solution.py:260
  314.2 0.0 copy-done
  314.3 0.6 reduce_sum.29
  314.9 0.0 copy-done.1
  314.9 0.6 reduce_sum.28
  316.8 0.0 copy-done.2
  316.8 0.6 reduce_sum.38
  317.5 0.0 copy-done.3
  317.5 0.6 reduce_sum.37
  319.4 0.7 broadcast_select_fusion.own_ref
  320.1 22.0 %shard_map.92 = f32[8,128]{1,0:T(8,128)} custom-call(f32[8,128]{1,0:T(8,128)} %broadcast_select_fusion.own_ref), custom_call_target="tpu_custom_call" | custom-call | tf_op jit(solution)/shard_map/pallas_call | solution.py:245
  342.1 1.3 multiply_reduce_fusion
  343.4 0.0 all-to-all-done.5
  343.4 2.4 convert_element_type.47.re_ref.im_ref
  345.9 4.8 %shard_map.91 = (f32[16,64,512]{2,1,0:T(8,128)}, f32[16,64,512]{2,1,0:T(8,128)}) custom-call(f32[1]{0:T(128)} %bitcast.6.scale_ref, f32[4,32,64,128]{3,2,1,0:T(8,128)} %convert_element_type.47.re_ref.im_ref, f32[4,32,64,128]{3,2,1,0:T(8,128)} %convert_element_type.47.re_ref.im_ref), custom_call_target="tpu_custom_call" | custom-call | tf_op jit(solution)/shard_map/pallas_call | solution.py:279
  (2 shorter events, 0.0 us)
Async XLA Ops:
  7.2 87.8 %all-gather.7.cloned.1.call-start = ((), (), s32[]{:S(2)}) async-start(), calls=%async_computation.7 | async-start | bytes 9437184 | tf_op jit(solution)/shard_map/all_gather | solution.py:302
  10.0 167.7 %all-gather.5.cloned.1.call-start = ((), (), s32[]{:S(2)}) async-start(), calls=%async_computation.6 | async-start | bytes 9437184 | tf_op jit(solution)/shard_map/all_gather | solution.py:302
  108.3 82.5 %all-to-all-start.1 = ((f16[4,2,8,64,128]{4,3,2,1,0:T(8,128)(2,1)}), f16[4,2,8,64,128]{4,3,2,1,0:T(8,128)(2,1)S(1)}, u32[]{:S(2)}, u32[]{:S(2)}) async-start(f16[4,2,8,64,128]{4,3,2,1,0:T(8,128)(2,1)} %convert_element_type.38), calls=%async_computation.1 | async-start | bytes 2097152 | tf_op jit(solution)/shard_map/all_to_all | solution.py:260
  190.9 17.8 %all-to-all-start = ((f16[4,2,8,64,128]{4,3,2,1,0:T(8,128)(2,1)}), f16[4,2,8,64,128]{4,3,2,1,0:T(8,128)(2,1)S(1)}, u32[]{:S(2)}, u32[]{:S(2)}) async-start(f16[4,2,8,64,128]{4,3,2,1,0:T(8,128)(2,1)} %convert_element_type.36), calls=%async_computation | async-start | bytes 2097152 | tf_op jit(solution)/shard_map/all_to_all | solution.py:260
  265.8 16.8 %all-to-all-start.4 = ((f16[4,2,8,64,128]{4,3,2,1,0:T(8,128)(2,1)}), f16[4,2,8,64,128]{4,3,2,1,0:T(8,128)(2,1)S(1)}, u32[]{:S(2)}, u32[]{:S(2)}) async-start(f16[4,2,8,64,128]{4,3,2,1,0:T(8,128)(2,1)} %multiply_convert_fusion), calls=%async_computation.4 | async-start | bytes 2097152 | tf_op jit(solution)/shard_map/all_to_all | solution.py:260
  282.6 15.6 %all-to-all-start.3 = ((f16[4,2,8,64,128]{4,3,2,1,0:T(8,128)(2,1)}), f16[4,2,8,64,128]{4,3,2,1,0:T(8,128)(2,1)S(1)}, u32[]{:S(2)}, u32[]{:S(2)}) async-start(f16[4,2,8,64,128]{4,3,2,1,0:T(8,128)(2,1)} %multiply_convert_fusion.1), calls=%async_computation.3 | async-start | bytes 2097152 | tf_op jit(solution)/shard_map/all_to_all | solution.py:260
  310.5 3.8 %copy-start = (f32[8,1,512]{2,1,0:T(1,128)S(1)}, f32[8,1,512]{2,1,0:T(1,128)}, u32[]{:S(2)}) copy-start(f32[8,1,512]{2,1,0:T(1,128)} %get-tuple-element.20) | copy-start | bytes 49156
  310.5 4.4 %copy-start.1 = (f32[8,1,512]{2,1,0:T(1,128)S(1)}, f32[8,1,512]{2,1,0:T(1,128)}, u32[]{:S(2)}) copy-start(f32[8,1,512]{2,1,0:T(1,128)} %get-tuple-element.19) | copy-start | bytes 49156
  310.5 6.4 %copy-start.2 = (f32[8,1,512]{2,1,0:T(1,128)S(1)}, f32[8,1,512]{2,1,0:T(1,128)}, u32[]{:S(2)}) copy-start(f32[8,1,512]{2,1,0:T(1,128)} %get-tuple-element.22) | copy-start | bytes 49156
  310.5 7.0 %copy-start.3 = (f32[8,1,512]{2,1,0:T(1,128)S(1)}, f32[8,1,512]{2,1,0:T(1,128)}, u32[]{:S(2)}) copy-start(f32[8,1,512]{2,1,0:T(1,128)} %get-tuple-element.21) | copy-start | bytes 49156
  310.5 33.0 %all-to-all-start.5 = ((f16[4,32,64,128]{3,2,1,0:T(8,128)(2,1)}), f16[4,32,64,128]{3,2,1,0:T(8,128)(2,1)S(1)}, u32[]{:S(2)}, u32[]{:S(2)}) async-start(f16[4,32,64,128]{3,2,1,0:T(8,128)(2,1)} %convert_element_type.46), calls=%async_computation.5 | async-start | bytes 4194304 | tf_op jit(solution)/shard_map/all_to_all | solution.py:260
Sparse Core Ops, SparseCore 0:
  10.1 84.7 all-gather.6
  97.1 80.5 all-gather.4
